TPU v7x, 32 devices: a whole 2x2x4 slice. The times are simulated.
32 devices in a mesh: aa: 4 (over x, core), ba: 8 (over z, y).
Axes of the slice: x: 2, y: 2, z: 4, core: 2. Of those that a mesh axis runs over, the one named last changes fastest.
Arguments:
- head_outputs: bfloat16 [1024, 4096], P('ba'), may hold values from -6 to 6
- stream: bfloat16 [1024, 4096], P('ba'), may hold values from -6 to 6
- adapter_down_factors: bfloat16 [4096, 512], P(None, 'aa'), may hold values from -0.09375 to 0.09375
- adapter_up_factors: bfloat16 [512, 4096], P('aa'), may hold values from -1.5 to 1.5
- norm_gain_vector: float32 [4096], replicated, may hold values from 0.5 to 1.5
- router_matrix: bfloat16 [4096, 8], replicated, may hold values from -0.09375 to 0.09375
- token_adapter_index: int32 [1024], P('ba'), may hold values from 0 to 31
- token_expert_index: int32 [1024, 2], P('ba'), may hold values from 0 to 7, all different within a row; in each aligned block of 128 rows (0 to 127, 128 to 255, ...) at most 48 rows name the same one
- gate_weight: bfloat16 [8, 4096, 14336], P('ba', None, 'aa'), may hold values from -0.09375 to 0.09375
- up_weight: bfloat16 [8, 4096, 14336], P('ba', None, 'aa'), may hold values from -0.09375 to 0.09375
- down_weight: bfloat16 [8, 14336, 4096], P('ba', 'aa'), may hold values from -0.046875 to 0.046875
Outputs:
- mixed: bfloat16 [1024, 4096], P('ba', 'aa')
- adapter_load: float32 [32], P('aa')
Inputs may be any that keep to these rules, and one draw needn't show every extreme that they name: `token_expert_index`: the two experts of a row differ; in each aligned block of 128 rows no expert is named by more than 48 rows.
All inputs are finite; a program needn't handle non-finite values.
Results may differ from a plain program's by a relative error of at most 0.0049.
Values may be sent and summed in bfloat16 or wider, within the bound.
No kernel may reach another device: no remote copies, remote signals or barrier semaphores. Data moves between devices by JAX's collectives and lax.ppermute only.
A program may use at most 192 MiB of HBM per device.

v0:
```python
import jax
import jax.numpy as jnp
from jax import lax
from jax.sharding import PartitionSpec as P

E = 8
ADAPTER_RANK = 16
CAP = 48


EPS = 1e-05
ADAPTER_SCALE = 2.0


def shards(
    head_outputs,
    stream,
    adapter_down_factors,
    adapter_up_factors,
    norm_gain_vector,
    router_matrix,
    token_adapter_index,
    token_expert_index,
    gate_weight,
    up_weight,
    down_weight,
):
    tok_rows = head_outputs.shape[0]
    model_width = head_outputs.shape[1]
    held_count = adapter_down_factors.shape[1] // ADAPTER_RANK
    groups = lax.axis_size("aa")
    index_aa = lax.axis_index("aa")
    local_ids = token_adapter_index - index_aa * held_count
    column_holder = jnp.arange(adapter_down_factors.shape[1], dtype=jnp.int32) // ADAPTER_RANK
    rank_projected = jnp.dot(head_outputs, adapter_down_factors, preferred_element_type=jnp.float32)
    rank_projected = jnp.where(
        local_ids[:, None] == column_holder[None, :], rank_projected, 0.0
    ).astype(jnp.bfloat16)
    partial_update = ADAPTER_SCALE * jnp.dot(
        rank_projected, adapter_up_factors, preferred_element_type=jnp.float32
    )
    tallies = jnp.sum(
        (local_ids[:, None] == jnp.arange(held_count, dtype=jnp.int32)[None, :]).astype(
            jnp.float32
        ),
        axis=0,
    )
    adapter_load = lax.psum(tallies, "ba")
    share_width = model_width // groups
    adapter_update = lax.psum(partial_update, "aa")
    residual_stream = stream.astype(jnp.float32) + adapter_update
    inv_norm = lax.rsqrt(jnp.mean(residual_stream * residual_stream, axis=1, keepdims=True) + EPS)
    normed = (residual_stream * inv_norm * norm_gain_vector).astype(jnp.bfloat16)
    residual_share = lax.dynamic_slice_in_dim(
        residual_stream, index_aa * share_width, share_width, 1
    )
    logits = jnp.dot(normed, router_matrix, preferred_element_type=jnp.float32)
    experts_iota = jnp.arange(E, dtype=jnp.int32)
    chosen = (token_expert_index[:, :, None] == experts_iota[None, None, :]).astype(jnp.float32)
    picked = jnp.sum(chosen * logits[:, None, :], axis=2)
    weights = 1.0 / (1.0 + jnp.exp(picked[:, ::-1] - picked))
    flat_experts = token_expert_index.reshape(-1)
    expert_hits = (flat_experts[:, None] == experts_iota[None, :]).astype(jnp.int32)
    before = jnp.cumsum(expert_hits, axis=0) - expert_hits
    slot_index = flat_experts * CAP + jnp.sum(before * expert_hits, axis=1)
    slots_iota = jnp.arange(E * CAP, dtype=jnp.int32)
    placed = slot_index[None, :] == slots_iota[:, None]
    pick_rows = jnp.sum(placed.astype(jnp.float32).reshape(E * CAP, tok_rows, 2), axis=2).astype(
        jnp.bfloat16
    )
    outgoing = jnp.dot(pick_rows, normed, preferred_element_type=jnp.float32).astype(jnp.bfloat16)
    halves = lax.axis_size("ba") // E
    outgoing = jnp.repeat(outgoing.reshape(E, CAP, model_width), halves, axis=0)
    mixing = jnp.where(placed, weights.reshape(1, -1), 0.0)
    mixing = jnp.sum(mixing.reshape(E * CAP, tok_rows, 2), axis=2)
    received = lax.all_to_all(outgoing, "ba", split_axis=0, concat_axis=0, tiled=True)
    sources = received.shape[0]
    items = received.shape[1]
    flat_rows = received.reshape(sources * items, model_width)
    gate_proj = jnp.dot(flat_rows, gate_weight[0], preferred_element_type=jnp.float32)
    up_proj = jnp.dot(flat_rows, up_weight[0], preferred_element_type=jnp.float32)
    hidden = (jax.nn.silu(gate_proj) * up_proj).astype(jnp.bfloat16)
    partial_value = jnp.dot(hidden, down_weight[0], preferred_element_type=jnp.float32).reshape(
        sources, items, model_width
    )
    reduced = lax.psum_scatter(partial_value, "aa", scatter_dimension=2, tiled=True)
    returned = lax.all_to_all(reduced, "ba", split_axis=0, concat_axis=0, tiled=True)
    summed = jnp.sum(returned.reshape(E, halves, CAP, returned.shape[2]), axis=1).reshape(
        E * CAP, returned.shape[2]
    )
    gathered = jnp.einsum("sr,sd->rd", mixing, summed, precision=lax.Precision.HIGHEST)
    mixed_share = residual_share + gathered
    return (mixed_share.astype(jnp.bfloat16), adapter_load)


def solution(mesh):
    in_specs = (
        P("ba", None),
        P("ba", None),
        P(None, "aa"),
        P("aa", None),
        P(),
        P(),
        P("ba"),
        P("ba", None),
        P("ba", None, "aa"),
        P("ba", None, "aa"),
        P("ba", "aa", None),
    )
    out_specs = (P("ba", "aa"), P("aa"))
    return jax.shard_map(shards, mesh=mesh, in_specs=in_specs, out_specs=out_specs, check_vma=False)
```

profile of v0, /device:TPU:8, one launch (start us, length us, event | category | flops | bytes accessed | tf_op | source)
XLA Modules:
  0.0 317.9 jit_solution(642658996399779848)
XLA Ops:
  7.2 0.0 copy-start
  7.2 0.0 all-reduce.2.cloned.1.call-start
  7.2 0.7 and_select_fusion
  8.0 0.4 copy-done
  8.4 0.0 copy-start.5
  8.4 3.6 %convolution_multiply_fusion = f32[128,4096]{1,0:T(8,128)} fusion(bf16[128,4096]{1,0:T(8,128)(2,1)S(1)} %copy-done, bf16[128,4096]{1,0:T(8,128)(2,1)} %param.11, bf16[4096,128]{1,0:T(8,128)(2,1)} %param.13, s32[128]{0:T(128)S(1)} %get-tuple-element.6, s32[128]{0:T(128)S(1)} %get-tuple-element.7), kind=kOutput, calls=%fused_computation.9 | convolution fusion | flops 269008896 | bytes 5243904 | tf_op jit(solution)/shard_map/dot_general | solution.py:39
  12.1 0.0 copy-start.2
  12.1 0.0 all-reduce.2.cloned.1.call-update
  12.1 0.0 copy-start.3
  12.1 0.0 copy-start.4
  12.1 0.0 reduce-scatter.2.cloned.1.call-start
  12.2 0.0 copy-done.5
  12.2 0.1 copy.27
  12.3 0.1 eq.86
  12.4 0.1 eq.82
  12.6 0.6 reduce-window.6
  13.2 0.2 slice_reduce_fusion
  13.4 0.1 fusion.20
  13.5 0.1 reduce_sum.61
  13.7 0.1 copy.29
  13.7 51.0 %all-reduce.2.cloned.1.call-done = f32[128,4096]{1,0:T(8,128)} async-done(((f32[128,4096]{1,0:T(8,128)}), f32[128,4096]{1,0:T(8,128)}) %all-reduce.2.cloned.1.call-update) | async-done | bytes 2097168 | tf_op jit(solution)/shard_map/psum | solution.py:50
  64.8 0.0 copy-done.2
  64.8 2.0 multiply_reduce_fusion
  66.8 0.0 copy-done.3
  66.8 0.0 copy-done.4
  66.8 0.4 fusion.23
  67.3 0.1 convert_reduce_fusion
  67.4 1.0 convolution_convert_fusion
  68.5 75.4 %all_to_all.10 = bf16[8,48,4096]{2,1,0:T(8,128)(2,1)S(1)} all-to-all(bf16[8,48,4096]{2,1,0:T(8,128)(2,1)S(1)} %bitcast.36), channel_id=1, replica_groups=mesh['aa'=4,'ba'=8] {'ba'}, dimensions={0} | all-to-all | bytes 6291456 | tf_op jit(solution)/shard_map/all_to_all | solution.py:76
  143.9 17.6 %fusion.4 = f32[384,3584]{1,0:T(8,128)} fusion(bf16[384,4096]{1,0:T(8,128)(2,1)S(1)} %bitcast.37, bf16[1,4096,3584]{2,1,0:T(8,128)(2,1)} %param.19), kind=kOutput, calls=%fused_computation.4 | convolution fusion | flops 11274289152 | bytes 38010880 | tf_op jit(solution)/shard_map/dot_general | solution.py:80
  161.5 19.0 %fusion.9 = bf16[384,3584]{1,0:T(8,128)(2,1)} fusion(bf16[384,4096]{1,0:T(8,128)(2,1)S(1)} %bitcast.38, bf16[1,4096,3584]{2,1,0:T(8,128)(2,1)} %param.20, f32[384,3584]{1,0:T(8,128)} %fusion.4), kind=kOutput, calls=%fused_computation.7 | convolution fusion | flops 11282546688 | bytes 40763392 | tf_op jit(solution)/shard_map/dot_general | solution.py:81
  180.5 19.3 %fusion = f32[8,48,4096]{2,1,0:T(8,128)} fusion(bf16[8,48,3584]{2,1,0:T(8,128)(2,1)} %bitcast.39, bf16[1,3584,4096]{2,1,0:T(8,128)(2,1)} %param.21), kind=kOutput, calls=%fused_computation | convolution fusion | flops 11274289152 | bytes 38404096 | tf_op jit(solution)/shard_map/dot_general | solution.py:83
  199.8 0.0 reduce-scatter.2.cloned.1.call-update
  199.9 0.0 copy-start.1
  199.9 56.7 %reduce-scatter.2.cloned.1.call-done = f32[8,48,1024]{2,1,0:T(8,128)} async-done(((f32[8,48,4096]{2,1,0:T(8,128)}), f32[8,48,1024]{2,1,0:T(8,128)}) %reduce-scatter.2.cloned.1.call-update) | async-done | bytes 1572880 | tf_op jit(solution)/shard_map/reduce_scatter | solution.py:86
  256.6 6.0 %all-to-all-start.1 = ((f32[8,48,1024]{2,1,0:T(8,128)}), f32[8,48,1024]{2,1,0:T(8,128)}, u32[]{:S(2)}, u32[]{:S(2)}) async-start(f32[8,48,1024]{2,1,0:T(8,128)} %reduce-scatter.2.cloned.1.call-done), calls=%async_computation.2 | async-start | bytes 3145728 | tf_op jit(solution)/shard_map/all_to_all | solution.py:87
  262.6 0.1 convert_reduce_fusion.1
  262.8 45.0 %psum.15 = f32[8]{0:T(128)} all-reduce(f32[8]{0:T(128)S(1)} %convert_reduce_fusion.1), channel_id=1, replica_groups=mesh['aa'=4,'ba'=8] {'ba'}, use_global_device_ids=true, to_apply=%region_10.11 | all-reduce | flops 8 | bytes 64 | tf_op jit(solution)/shard_map/psum | solution.py:48
  307.8 0.0 all-to-all-done.1
  307.8 3.2 %fusion.12 = bf16[128,1024]{1,0:T(8,128)(2,1)} fusion(f32[384,128]{1,0:T(8,128)S(1)} %get-tuple-element.3, f32[384,1024]{1,0:T(8,128)} %bitcast.9, f32[128,4096]{1,0:T(8,128)S(1)} %get-tuple-element.5, s32[]{:T(128)S(6)} %select_n.23), kind=kOutput, calls=%fused_computation.14 | convolution fusion | flops 604241920 | bytes 2555908 | tf_op jit(solution)/shard_map/sr,sd->rd/dot_general | solution.py:91
  311.0 0.0 copy-done.1
  (8 shorter events, 0.1 us)
Async XLA Ops:
  7.2 1.2 copy-start
  7.2 57.6 %all-reduce.2.cloned.1.call-start = ((), (), s32[]{:S(2)}) async-start(), calls=%async_computation.3 | async-start | bytes 4194304 | tf_op jit(solution)/shard_map/psum | solution.py:50
  8.4 3.7 %copy-start.5 = (s32[128,2]{0,1:T(2,128)S(1)}, s32[128,2]{0,1:T(2,128)}, u32[]{:S(2)}) copy-start(s32[128,2]{0,1:T(2,128)} %param.18) | copy-start | bytes 3076
  12.1 52.7 %copy-start.2 = (bf16[128,4096]{1,0:T(8,128)(2,1)S(1)}, bf16[128,4096]{1,0:T(8,128)(2,1)}, u32[]{:S(2)}) copy-start(bf16[128,4096]{1,0:T(8,128)(2,1)} %param.12) | copy-start | bytes 3145732
  12.1 54.7 %copy-start.3 = (f32[4096]{0:T(1024)S(1)}, f32[4096]{0:T(1024)}, u32[]{:S(2)}) copy-start(f32[4096]{0:T(1024)} %param.15) | copy-start | bytes 49156
  12.1 54.7 %copy-start.4 = (bf16[4096,8]{0,1:T(8,128)(2,1)S(1)}, bf16[4096,8]{0,1:T(8,128)(2,1)}, u32[]{:S(2)}) copy-start(bf16[4096,8]{0,1:T(8,128)(2,1)} %param.16) | copy-start | bytes 196612
  12.1 244.5 %reduce-scatter.2.cloned.1.call-start = ((), (), s32[]{:S(2)}) async-start(), calls=%async_computation.4 | async-start | bytes 7864320 | tf_op jit(solution)/shard_map/reduce_scatter | solution.py:86
  199.9 111.2 %copy-start.1 = (bf16[128,4096]{1,0:T(8,128)(2,1)S(1)}, bf16[128,4096]{1,0:T(8,128)(2,1)}, u32[]{:S(2)}) copy-start(bf16[128,4096]{1,0:T(8,128)(2,1)} %param.14) | copy-start | bytes 3145732
  256.6 51.2 %all-to-all-start.1 = ((f32[8,48,1024]{2,1,0:T(8,128)}), f32[8,48,1024]{2,1,0:T(8,128)}, u32[]{:S(2)}, u32[]{:S(2)}) async-start(f32[8,48,1024]{2,1,0:T(8,128)} %reduce-scatter.2.cloned.1.call-done), calls=%async_computation.2 | async-start | bytes 3145728 | tf_op jit(solution)/shard_map/all_to_all | solution.py:87
Sparse Core Ops, SparseCore 0:
  12.2 52.5 all-reduce.1
  200.0 56.5 reduce-scatter.1
where the time goes:
time: 318 us
  blocking collectives  120 us (38%)
  waiting for transfers between devices  108 us (34%)
  matrix products  64.3 us (20%)
  between operations  14.2 us (4%)
  starting transfers between devices  6.13 us (2%)
  other arithmetic  3.7 us (1%)
    all_to_all x1, blocking collectives, shards(): lax.all_to_all(outgoing, 'ba', split_axis=0, concat_axis=0, tiled=True)  75.4 us
    reduce_scatter x1, waiting for transfers between devices, shards(): lax.psum_scatter(partial_value, 'aa', scatter_dimension=2, tiled=True)  56.7 us
    psum x1, waiting for transfers between devices, shards(): adapter_update = lax.psum(partial_update, 'aa')  51 us
    psum x1, blocking collectives, shards(): adapter_load = lax.psum(tallies, 'ba')  45 us
    dot_general x1, matrix products, shards(): jnp.dot(hidden, down_weight[0], preferred_element_type=jnp.float32)  19.3 us
    dot_general x1, matrix products, shards(): jnp.dot(flat_rows, up_weight[0], preferred_element_type=jnp.float32)  19 us
    dot_general x1, matrix products, shards(): jnp.dot(flat_rows, gate_weight[0], preferred_element_type=jnp.float32)  17.6 us
  transfers between devices with their start and end apart: 3, of which 2 were waited for; matrix products, arithmetic and copies ran while one was open for 1% of the time, Pallas kernels for 0%

commit v1 on v0

v1 whole, which is shorter than its diff:
```python
import functools

import jax
import jax.numpy as jnp
from jax import lax
from jax.experimental import pallas as pl
from jax.experimental.pallas import tpu as pltpu
from jax.sharding import PartitionSpec as P


ADAPTER_RANK = 16
CAP = 48

EPS = 1e-05
ADAPTER_SCALE = 2.0
LANES = 128
RING = 6


def swap(value, axis, distance):
    size = lax.axis_size(axis)
    return lax.ppermute(value, axis, [(k, k ^ distance) for k in range(size)])


def tile_of(width, most):
    tile = most
    while width % tile:
        tile //= 2
    return tile


def expert_kernel(offset_ref, gain_hbm, *refs, groups, rows_of, owners):
    count = len(rows_of)
    number_of_groups = len(groups)
    pieces, refs = refs[:count], refs[count:]
    gate_ref, up_ref, down_ref = refs[:3]
    send_refs = refs[3 : 3 + number_of_groups]
    keep_refs = refs[3 + number_of_groups : 3 + 2 * number_of_groups]
    x_ref, hidden_ref, inv_ref, gain_ref, ring_ref, piece_sem, ring_sem = refs[
        3 + 2 * number_of_groups :
    ]
    total_rows, model_width = x_ref.shape
    hidden_width = hidden_ref.shape[1]
    slots, _, tile = ring_ref.shape
    width = model_width // owners
    share = width // tile
    pairs = hidden_width // tile
    down_tiles = model_width // tile
    sends = down_tiles // 2
    ahead = slots // 2

    def gate_copy(n):
        slot = (2 * n) % slots
        return pltpu.make_async_copy(
            gate_ref.at[0, :, pl.ds(n * tile, tile)], ring_ref.at[slot], ring_sem.at[slot]
        )

    def up_copy(n):
        slot = (2 * n + 1) % slots
        return pltpu.make_async_copy(
            up_ref.at[0, :, pl.ds(n * tile, tile)], ring_ref.at[slot], ring_sem.at[slot]
        )

    def down_copy(d):
        slot = (2 * pairs + d) % slots
        order = d // share
        index = jnp.where(d < sends, 2 * order + 1, 2 * (order - owners // 2))
        column = offset_ref[index] * share + d % share
        return pltpu.make_async_copy(
            down_ref.at[0, :, pl.ds(column * tile, tile)],
            ring_ref.at[slot, pl.ds(0, hidden_width), :],
            ring_sem.at[slot],
        )

    copies = [pltpu.make_async_copy(gain_hbm, gain_ref, piece_sem.at[count])]
    for number, piece in enumerate(pieces):
        first, index = rows_of[number]
        start = pl.multiple_of(offset_ref[index] * width, LANES)
        copies.append(
            pltpu.make_async_copy(
                piece,
                x_ref.at[pl.ds(first, piece.shape[0]), pl.ds(start, width)],
                piece_sem.at[number],
            )
        )
    for copy in copies:
        copy.start()
    for n in range(ahead):
        if n < pairs:
            gate_copy(n).start()
            up_copy(n).start()
        else:
            down_copy(2 * (n - pairs)).start()
            down_copy(2 * (n - pairs) + 1).start()
    for copy in copies:
        copy.wait()

    chunk = 16
    gain_ref[...] = 1.0 / gain_ref[...]

    def norm_step(c, carry):
        rows = pl.ds(pl.multiple_of(c * chunk, chunk), chunk)
        values = x_ref[rows, :].astype(jnp.float32) * gain_ref[...]
        mean = jnp.sum(values * values, axis=1, keepdims=True) / model_width
        inv_ref[rows, :] = jnp.broadcast_to(lax.rsqrt(mean + EPS), (chunk, LANES))
        return carry

    lax.fori_loop(0, total_rows // chunk, norm_step, 0)

    def pair_step(n, carry):
        rows = x_ref[...]
        inv = inv_ref[:, :1]
        gate_copy(n).wait()
        up_copy(n).wait()
        gate = jnp.dot(rows, ring_ref[(2 * n) % slots], preferred_element_type=jnp.float32)
        up = jnp.dot(rows, ring_ref[(2 * n + 1) % slots], preferred_element_type=jnp.float32)
        gate = gate * inv
        value = (gate / (1.0 + jnp.exp(-gate))) * (up * inv)
        hidden_ref[:, pl.ds(pl.multiple_of(n * tile, tile), tile)] = value.astype(jnp.bfloat16)
        later = n + ahead

        @pl.when(later < pairs)
        def _():
            gate_copy(later).start()
            up_copy(later).start()

        @pl.when((later >= pairs) & (2 * (later - pairs) < down_tiles))
        def _():
            down_copy(2 * (later - pairs)).start()
            down_copy(2 * (later - pairs) + 1).start()

        return carry

    lax.fori_loop(0, pairs, pair_step, 0)

    def phase(base, out_refs):
        def down_step(d, carry):
            slot = (2 * pairs + base + d) % slots
            down_copy(base + d).wait()
            part = jnp.dot(
                hidden_ref[...],
                ring_ref[slot, pl.ds(0, hidden_width), :],
                preferred_element_type=jnp.float32,
            )
            start = pl.multiple_of((d % share) * tile, tile)
            for out_ref, (first, rows) in zip(out_refs, groups):
                out_ref[d // share, :, pl.ds(start, tile)] = part[first : first + rows].astype(
                    out_ref.dtype
                )
            later = base + d + 2 * ahead

            @pl.when(later < down_tiles)
            def _():
                down_copy(later).start()

            return carry

        lax.fori_loop(0, sends, down_step, 0)

    phase(0, send_refs)
    phase(sends, keep_refs)


def expert_rows(pieces, rows_of, groups, offsets, gain, gate_weight, up_weight, down_weight):
    model_width, hidden_width = gate_weight.shape[1:]
    owners = offsets.shape[0]
    width = model_width // owners
    total_rows = sum(rows for _, rows in groups)
    tile = tile_of(hidden_width, 512)
    while width % tile or ((model_width // tile) // 2) % 2:
        tile //= 2
    bf16, f32 = jnp.bfloat16, jnp.float32
    return pl.pallas_call(
        functools.partial(expert_kernel, groups=groups, rows_of=rows_of, owners=owners),
        out_shape=[jax.ShapeDtypeStruct((owners // 2, rows, width), bf16) for _, rows in groups]
        + [jax.ShapeDtypeStruct((owners // 2, rows, width), f32) for _, rows in groups],
        in_specs=[pl.BlockSpec(memory_space=pltpu.SMEM), pl.BlockSpec(memory_space=pltpu.HBM)]
        + [pl.BlockSpec(memory_space=pl.ANY)] * len(pieces)
        + [pl.BlockSpec(memory_space=pltpu.HBM)] * 3,
        out_specs=[pl.BlockSpec(memory_space=pltpu.VMEM)] * (2 * len(groups)),
        scratch_shapes=[
            pltpu.VMEM((total_rows, model_width), bf16),
            pltpu.VMEM((total_rows, hidden_width), bf16),
            pltpu.VMEM((total_rows, LANES), f32),
            pltpu.VMEM((1, model_width), f32),
            pltpu.VMEM((RING, model_width, tile), bf16),
            pltpu.SemaphoreType.DMA((len(pieces) + 1,)),
            pltpu.SemaphoreType.DMA((RING,)),
        ],
        compiler_params=pltpu.CompilerParams(vmem_limit_bytes=45 << 20),
        name="expert_rows",
    )(offsets, gain, *pieces, gate_weight, up_weight, down_weight)


def with_adapter(rows, up_refs, spread_ref, adapter_ref, width):
    held = up_refs[0].shape[0]
    low = rows[:, width : width + ADAPTER_RANK]
    ids = rows[:, width + ADAPTER_RANK : width + ADAPTER_RANK + 1].astype(jnp.float32)
    wide = jnp.dot(low, spread_ref[...], preferred_element_type=jnp.float32)
    wide = jnp.where(ids == adapter_ref[...].astype(jnp.float32), wide, 0.0).astype(jnp.bfloat16)
    update = sum(
        jnp.dot(wide[:, k * held : (k + 1) * held], up[...], preferred_element_type=jnp.float32)
        for k, up in enumerate(up_refs)
    )
    return rows[:, :width].astype(jnp.float32) + ADAPTER_SCALE * update


def adapter_kernel(*refs, blocks):
    block_refs, up_refs = refs[:blocks], refs[blocks:-4]
    spread_ref, adapter_ref, gain_ref, out_ref = refs[-4:]
    width = out_ref.shape[1]
    rows = jnp.concatenate([block[...] for block in block_refs], axis=0)
    total = with_adapter(rows, up_refs, spread_ref, adapter_ref, width)
    out_ref[...] = (total * gain_ref[...]).astype(jnp.bfloat16)


def adapter_rows(blocks, up_parts, spread, adapter_of, gain):
    rows = sum(block.shape[0] for block in blocks)
    return pl.pallas_call(
        functools.partial(adapter_kernel, blocks=len(blocks)),
        out_shape=jax.ShapeDtypeStruct((rows, gain.shape[1]), jnp.bfloat16),
        compiler_params=pltpu.CompilerParams(vmem_limit_bytes=16 << 20),
        name="adapter_rows",
    )(*blocks, *up_parts, spread, adapter_of, gain)


def total_kernel(keep_ref, other_ref, *refs, count):
    part_refs, out_refs = refs[:count], refs[count:]
    rows = out_refs[0].shape[0]
    for k, out_ref in enumerate(out_refs):
        span = pl.ds(k * rows, rows)
        total = keep_ref[0, span, :] + other_ref[0, span, :].astype(jnp.float32)
        for part_ref in part_refs:
            total = total + part_ref[span, :].astype(jnp.float32)
        out_ref[...] = total.astype(jnp.bfloat16)


def total_rows_of(keep, other, parts, blocks):
    _, rows, width = keep.shape
    first = pl.BlockSpec((1, rows, width), lambda n: (0, 0, 0))
    whole = pl.BlockSpec((rows, width), lambda n: (0, 0))
    block = pl.BlockSpec((rows // blocks, width), lambda n: (0, 0))
    return pl.pallas_call(
        functools.partial(total_kernel, count=len(parts)),
        grid=(1,),
        out_shape=[jax.ShapeDtypeStruct((rows // blocks, width), jnp.bfloat16)] * blocks,
        in_specs=[first, first] + [whole] * len(parts),
        out_specs=[block] * blocks,
        compiler_params=pltpu.CompilerParams(vmem_limit_bytes=16 << 20),
        name="total_rows",
    )(keep, other, *parts)


def column_copy(source, first, width, target, sem):
    start = pl.multiple_of(first * width, LANES)
    return pltpu.make_async_copy(source.at[:, pl.ds(start, width)], target, sem)


def ids_by_row(ids_row):
    tokens = ids_row.shape[1]
    return jnp.broadcast_to(ids_row.astype(jnp.float32), (LANES, tokens)).T


def front_kernel(
    place_ref, ids_ref, experts_ref, head_hbm, down_hbm, up_ref, stream_ref, *refs, owners, sizes
):
    low_ref, stream_out, pick_ref, extra_ref, target_ref = refs[:5]
    up_outs = refs[5:-3]
    head_ref, down_ref, sem = refs[-3:]
    width = stream_out.shape[1]
    held_width = down_ref.shape[1]
    owner = place_ref[0]
    first_copies = [
        pltpu.make_async_copy(head_hbm, head_ref, sem.at[owners + 1]),
        pltpu.make_async_copy(down_hbm, down_ref, sem.at[owners + 2]),
    ]
    copies = [column_copy(stream_ref, owner, width, stream_out, sem.at[owners])]
    for r, out in enumerate(up_outs):
        copies.append(column_copy(up_ref, owner ^ r, width, out, sem.at[r]))
    for copy in first_copies + copies:
        copy.start()
    f32, i32 = jnp.float32, jnp.int32
    experts, halves = sizes
    tokens = ids_ref.shape[1]
    ids = ids_by_row(ids_ref[...])
    lanes = lax.broadcasted_iota(i32, (tokens, LANES), 1)
    held = held_width // ADAPTER_RANK
    lane_held = lanes - 2 * ADAPTER_RANK
    wanted = jnp.where((lane_held >= 0) & (lane_held < held), owner * held + lane_held, -1)
    tally = jnp.sum(jnp.where(ids == wanted.astype(f32), 1.0, 0.0), axis=0, keepdims=True)
    extra_ref[0:tokens, :] = jnp.where(lanes == ADAPTER_RANK, ids, 0.0)
    extra_ref[tokens : tokens + 8, :] = jnp.broadcast_to(tally, (8, LANES))

    names = lax.broadcasted_iota(i32, (experts, tokens), 0)
    hits = [experts_ref[k : k + 1, :] == names for k in range(2)]
    both = jnp.where(hits[0] | hits[1], 1.0, 0.0)
    square = (tokens, tokens)
    earlier = lax.broadcasted_iota(i32, square, 0) < lax.broadcasted_iota(i32, square, 1)
    before = jnp.dot(
        both.astype(jnp.bfloat16),
        jnp.where(earlier, 1.0, 0.0).astype(jnp.bfloat16),
        preferred_element_type=f32,
    )
    targets, chosen = [], []
    for k in range(2):
        position = jnp.sum(jnp.where(hits[k], before, 0.0), axis=0, keepdims=True).astype(i32)
        chosen.append(experts_ref[k : k + 1, :].astype(f32))
        for half in range(halves):
            slot = (experts_ref[k : k + 1, :] * halves + half) ^ place_ref[1]
            targets.append(slot * CAP + position)
    rows = lax.broadcasted_iota(i32, pick_ref.shape, 0)
    pick = functools.reduce(jnp.logical_or, [rows == target for target in targets])
    pick_ref[...] = jnp.where(pick, 1.0, 0.0).astype(jnp.bfloat16)
    filled = jnp.zeros((LANES - len(targets) - 2, tokens), f32)
    target_ref[...] = jnp.concatenate(
        chosen + [target.astype(f32) for target in targets] + [filled], axis=0
    ).T
    for copy in first_copies:
        copy.wait()
    low = jnp.dot(head_ref[...], down_ref[...], preferred_element_type=jnp.float32)
    lane = lax.broadcasted_iota(jnp.int32, (low.shape[0], LANES), 1)
    first = owner * held
    masked = []
    for start in range(0, held_width, LANES):
        adapter = (first + (lane + start) // ADAPTER_RANK).astype(jnp.float32)
        masked.append(jnp.where(ids == adapter, low[:, start : start + LANES], 0.0))
    low = jnp.concatenate(masked, axis=1).astype(jnp.bfloat16)
    fold_shape = (ADAPTER_RANK, held_width)
    fold = lax.broadcasted_iota(jnp.int32, fold_shape, 1) % ADAPTER_RANK
    fold = jnp.where(fold == lax.broadcasted_iota(jnp.int32, fold_shape, 0), 1.0, 0.0)
    low_ref[...] = lax.dot_general(
        fold.astype(jnp.bfloat16),
        low,
        (((1,), (1,)), ((), ())),
        preferred_element_type=jnp.float32,
    ).astype(jnp.bfloat16)
    for copy in copies:
        copy.wait()


def front(place, head_outputs, down_factors, ids, experts_of, up_factors, stream, owners, sizes):
    rows, model_width = head_outputs.shape
    total_rows = sizes[0] * sizes[1] * CAP
    width = model_width // owners
    bf16 = jnp.bfloat16
    vmem, hbm = pl.BlockSpec(memory_space=pltpu.VMEM), pl.BlockSpec(memory_space=pltpu.HBM)
    return pl.pallas_call(
        functools.partial(front_kernel, owners=owners, sizes=sizes),
        out_shape=[
            jax.ShapeDtypeStruct((ADAPTER_RANK, rows), bf16),
            jax.ShapeDtypeStruct((rows, width), bf16),
            jax.ShapeDtypeStruct((total_rows, rows), bf16),
            jax.ShapeDtypeStruct((rows + 8, LANES), jnp.float32),
            jax.ShapeDtypeStruct((rows, LANES), jnp.float32),
        ]
        + [jax.ShapeDtypeStruct((up_factors.shape[0], width), bf16)] * owners,
        in_specs=[pl.BlockSpec(memory_space=pltpu.SMEM), vmem, vmem] + [hbm] * 4,
        out_specs=[vmem] * (5 + owners),
        scratch_shapes=[
            pltpu.VMEM(head_outputs.shape, bf16),
            pltpu.VMEM(down_factors.shape, bf16),
            pltpu.SemaphoreType.DMA((owners + 3,)),
        ],
        compiler_params=pltpu.CompilerParams(vmem_limit_bytes=52 << 20),
        name="front",
    )(place, ids[None, :], experts_of.T, head_outputs, down_factors, up_factors, stream)


def route_kernel(pick_ref, extra_ref, stream_ref, *refs, owners):
    low_refs, payload_ref, out_refs = refs[:owners], refs[owners], refs[owners + 1 :]
    f32, bf16 = jnp.float32, jnp.bfloat16
    tokens, width = stream_ref.shape
    low = sum(ref[...].astype(f32) for ref in low_refs)
    lows = jnp.concatenate([low, jnp.zeros((LANES - ADAPTER_RANK, tokens), f32)], axis=0).T
    extra = extra_ref[...]
    tail = (lows + extra[:tokens]).astype(bf16)
    tally = extra[tokens : tokens + 1]
    pick = pick_ref[...]
    payload_ref[:, pl.ds(0, width)] = stream_ref[...]
    payload_ref[:, pl.ds(width, LANES)] = tail

    moved = jnp.dot(pick, stream_ref[...], preferred_element_type=f32).astype(bf16)
    moved_tail = (jnp.dot(pick, tail, preferred_element_type=f32) + tally).astype(bf16)
    for s, out_ref in enumerate(out_refs):
        out_ref[:, pl.ds(0, width)] = moved[s * CAP : (s + 1) * CAP]
        out_ref[:, pl.ds(width, LANES)] = moved_tail[s * CAP : (s + 1) * CAP]


def route(pick, extra, stream_share, low_parts, peers):
    tokens, width = stream_share.shape
    bf16 = jnp.bfloat16
    vmem = pl.BlockSpec(memory_space=pltpu.VMEM)
    return pl.pallas_call(
        functools.partial(route_kernel, owners=len(low_parts)),
        out_shape=[jax.ShapeDtypeStruct((tokens, width + LANES), bf16)]
        + [jax.ShapeDtypeStruct((CAP, width + LANES), bf16)] * peers,
        in_specs=[vmem] * (3 + len(low_parts)),
        out_specs=[vmem] * (1 + peers),
        compiler_params=pltpu.CompilerParams(vmem_limit_bytes=16 << 20),
        name="route",
    )(pick, extra, stream_share, *low_parts)


def own_kernel(payload_ref, *refs):
    up_refs = refs[:-6]
    spread_ref, adapter_ref, gain_ref, router_ref, residual_ref, stats_ref = refs[-6:]
    rows = payload_ref[...]
    total = with_adapter(rows, up_refs, spread_ref, adapter_ref, gain_ref.shape[1])
    residual_ref[...] = total
    scaled = (total * gain_ref[...]).astype(jnp.bfloat16)
    squares = jnp.sum(total * total, axis=1, keepdims=True)
    logits = lax.dot_general(
        router_ref[...], scaled, (((1,), (1,)), ((), ())), preferred_element_type=jnp.float32
    )
    experts = logits.shape[0]
    stats_ref[0:experts, :] = logits
    squares = jnp.broadcast_to(squares, (squares.shape[0], LANES)).T
    stats_ref[experts : 2 * experts, :] = squares[:experts]


def own_rows(payload, up_parts, spread, adapter_of, gain, router):
    tokens, width = payload.shape[0], gain.shape[1]
    return pl.pallas_call(
        own_kernel,
        out_shape=[
            jax.ShapeDtypeStruct((tokens, width), jnp.float32),
            jax.ShapeDtypeStruct((2 * router.shape[0], tokens), jnp.float32),
        ],
        compiler_params=pltpu.CompilerParams(vmem_limit_bytes=16 << 20),
        name="own_rows",
    )(payload, *up_parts, spread, adapter_of, gain, router)


def mix_kernel(target_ref, *refs, blocks, halves, model_width):
    stat_refs, block_refs = refs[: -3 - blocks], refs[-3 - blocks : -3]
    high_ref, rest_ref, load_ref = refs[-3:]
    f32 = jnp.float32
    stats = sum(ref[...] for ref in stat_refs)
    count, tokens = stats.shape
    stats = jnp.concatenate([stats, jnp.zeros((LANES - count, tokens), f32)], axis=0).T
    inv = lax.rsqrt(stats[:, count // 2 : count // 2 + 1] / model_width + EPS)
    lane = lax.broadcasted_iota(jnp.int32, stats.shape, 1).astype(f32)
    picked = [
        jnp.sum(
            jnp.where(target_ref[:, k : k + 1] == lane, stats * inv, 0.0), axis=1, keepdims=True
        )
        for k in range(2)
    ]
    slots = lax.broadcasted_iota(jnp.int32, high_ref.shape, 1).astype(f32)
    mixing = jnp.zeros(high_ref.shape, f32)
    for k in range(2):
        weight = 1.0 / (1.0 + jnp.exp(picked[1 - k] - picked[k]))
        for half in range(halves):
            column = 2 + k * halves + half
            mixing = jnp.where(slots == target_ref[:, column : column + 1], weight, mixing)
    high = mixing.astype(jnp.bfloat16)
    high_ref[...] = high
    rest_ref[...] = (mixing - high.astype(f32)).astype(jnp.bfloat16)
    load_ref[...] = sum(ref[...].astype(f32)[:1, :] for ref in block_refs)


def mix(targets, stats, blocks, experts, model_width):
    tokens = targets.shape[0]
    peers = len(blocks)
    width = blocks[0].shape[1] - LANES
    total_rows = peers * CAP
    full = lambda shape: pl.BlockSpec(shape, lambda n: (0,) * len(shape))
    corner = pl.BlockSpec((16, LANES), lambda n: (0, width // LANES))
    return pl.pallas_call(
        functools.partial(
            mix_kernel, blocks=peers, halves=peers // experts, model_width=model_width
        ),
        grid=(1,),
        out_shape=[jax.ShapeDtypeStruct((tokens, total_rows), jnp.bfloat16)] * 2
        + [jax.ShapeDtypeStruct((1, LANES), jnp.float32)],
        in_specs=[full(targets.shape)]
        + [full(stat.shape) for stat in stats]
        + [corner] * peers,
        out_specs=[full((tokens, total_rows))] * 2 + [full((1, LANES))],
        compiler_params=pltpu.CompilerParams(vmem_limit_bytes=16 << 20),
        name="mix",
    )(targets, *stats, *blocks)


def finish_kernel(residual_ref, high_ref, rest_ref, *refs):
    block_refs, out_ref = refs[:-1], refs[-1]
    rows = jnp.concatenate([ref[...] for ref in block_refs], axis=0)
    total = jnp.dot(rest_ref[...], rows, preferred_element_type=jnp.float32)
    total = total + jnp.dot(high_ref[...], rows, preferred_element_type=jnp.float32)
    out_ref[...] = (residual_ref[...] + total).astype(out_ref.dtype)


def finish(residual, high, rest, blocks):
    return pl.pallas_call(
        finish_kernel,
        out_shape=jax.ShapeDtypeStruct(residual.shape, jnp.bfloat16),
        compiler_params=pltpu.CompilerParams(vmem_limit_bytes=16 << 20),
        name="finish",
    )(residual, high, rest, *blocks)


def shards(
    head_outputs,
    stream,
    adapter_down_factors,
    adapter_up_factors,
    norm_gain_vector,
    router_matrix,
    token_adapter_index,
    token_expert_index,
    gate_weight,
    up_weight,
    down_weight,
):
    _, model_width = head_outputs.shape
    held_width = adapter_down_factors.shape[1]
    held_count = held_width // ADAPTER_RANK
    experts = router_matrix.shape[1]
    owners = lax.axis_size("aa")
    peers = lax.axis_size("ba")
    index_aa = lax.axis_index("aa")
    index_ba = lax.axis_index("ba")
    width = model_width // owners
    f32, bf16, i32 = jnp.float32, jnp.bfloat16, jnp.int32

    place = jnp.stack([index_aa, index_ba])
    low, stream_share, pick, extra, targets, *up_parts = front(
        place,
        head_outputs,
        adapter_down_factors,
        token_adapter_index,
        token_expert_index,
        adapter_up_factors,
        stream,
        owners,
        (experts, peers // experts),
    )
    low_parts = [low] + [swap(low, "aa", r) for r in range(1, owners)]
    up_parts = [up_parts[0]] + [swap(up_parts[r], "aa", r) for r in range(1, owners)]
    spots = jnp.arange(owners * held_width, dtype=i32)
    adapter_of = (index_aa ^ (spots // held_width)) * held_count + (
        spots % held_width
    ) // ADAPTER_RANK
    adapter_of = adapter_of[None, :]
    spread = (jnp.arange(ADAPTER_RANK, dtype=i32)[:, None] == spots[None, :] % ADAPTER_RANK).astype(
        bf16
    )

    payload, *outgoing = route(pick, extra, stream_share, low_parts, peers)
    near = peers // 2
    split = near + near // 2
    received = [swap(block, "ba", s) if s else block for s, block in enumerate(outgoing)]

    gain = lax.dynamic_slice_in_dim(norm_gain_vector, index_aa * width, width, 0)[None, :]
    pieces, rows_of, groups = [], [], []
    spans = ((0, near), (near, split), (split, peers))
    for first, last in spans:
        own = adapter_rows(received[first:last], up_parts, spread, adapter_of, gain)
        held = [own] + [swap(own, "aa", r) for r in range(2, owners, 2)]
        groups.append((first * CAP, (last - first) * CAP))
        for number, piece in enumerate(held):
            pieces += [piece, swap(piece, "aa", 1)]
            rows_of += [(first * CAP, 2 * number), (first * CAP, 2 * number + 1)]

    router = lax.dynamic_slice_in_dim(router_matrix.T, index_aa * width, width, 1)
    residual_share, stats = own_rows(payload, up_parts, spread, adapter_of, gain, router)
    stats = [stats] + [swap(stats, "aa", r) for r in range(1, owners)]
    high, rest, load = mix(targets, stats, received, experts, model_width)
    adapter_load = load[0, 2 * ADAPTER_RANK : 2 * ADAPTER_RANK + held_count]

    offsets = index_aa ^ jnp.arange(owners, dtype=i32)
    results = expert_rows(
        pieces,
        tuple(rows_of),
        tuple(groups),
        offsets,
        norm_gain_vector[None, :],
        gate_weight,
        up_weight,
        down_weight,
    )

    returned = [None] * peers
    for g in (1, 2, 0):
        first, last = spans[g]
        send, keep = results[g], results[len(groups) + g]
        other = swap(send, "aa", 1)
        parts = [
            swap((keep[d] + other[d].astype(f32)).astype(bf16), "aa", 2 * d)
            for d in range(1, owners // 2)
        ]
        blocks = total_rows_of(keep, other, parts, last - first)
        for s, block in zip(range(first, last), blocks):
            returned[s] = swap(block, "ba", s) if s else block
    return (finish(residual_share, high, rest, returned), adapter_load)


def solution(mesh):
    in_specs = (
        P("ba", None),
        P("ba", None),
        P(None, "aa"),
        P("aa", None),
        P(),
        P(),
        P("ba"),
        P("ba", None),
        P("ba", None, "aa"),
        P("ba", None, "aa"),
        P("ba", "aa", None),
    )
    out_specs = (P("ba", "aa"), P("aa"))

    return jax.shard_map(shards, mesh=mesh, in_specs=in_specs, out_specs=out_specs, check_vma=False)
```

time: 318 us -> 142 us (0.45)
  blocking collectives: 120 us -> 0 us
  matrix products: 64.3 us -> 0 us
  waiting for transfers between devices: 108 us -> 53.4 us
  Pallas kernels: 0 us -> 49.7 us
  starting transfers between devices: 6.13 us -> 32 us
  between operations: 14.2 us -> 0.81 us
  other arithmetic: 3.7 us -> 0.27 us
    all_to_all x1 -> x0, blocking collectives: 75.4 us -> none  [shards(): lax.all_to_all(outgoing, 'ba', split_axis=0, concat_axis=0, tiled=True)]
    dot_general x7 -> x0, matrix products: 64.3 us -> none  [the longest x1 19.3 us: shards(): jnp.dot(hidden, down_weight[0], preferred_element_type=jnp.float32)]
    reduce_scatter x1 -> x0, waiting for transfers between devices: 56.7 us -> none  [shards(): lax.psum_scatter(partial_value, 'aa', scatter_dimension=2, tiled=True)]
    ppermute x0 -> x38, waiting for transfers between devices: none -> 53.4 us  [swap(): return lax.ppermute(value, axis, [(k, k ^ distance) for k in range(size)])]
    psum x1 -> x0, waiting for transfers between devices: 51 us -> none  [shards(): adapter_update = lax.psum(partial_update, 'aa')]
    pallas_call x0 -> x12, Pallas kernels: none -> 49.7 us  [the longest x1 42.4 us: expert_rows(): pl.pallas_call(functools.partial(expert_kernel, groups=groups, rows_of=ro...]
    psum x1 -> x0, blocking collectives: 45 us -> none  [shards(): adapter_load = lax.psum(tallies, 'ba')]
    ppermute x0 -> x38, starting transfers between devices: none -> 32 us  [swap(): return lax.ppermute(value, axis, [(k, k ^ distance) for k in range(size)])]
  transfers between devices with their start and end apart: 3 -> 38, of which waited for: 2 -> 19; matrix products, arithmetic and copies ran while one was open for 1% -> 1% of each run, Pallas kernels for 0% -> 2%
where the time goes in v1:
time: 142 us; the launch traced here: 139 us
  waiting for transfers between devices  53.4 us (38%)
  Pallas kernels  49.7 us (35%)
  starting transfers between devices  32 us (23%)
  local copies, waits for them, and re-layouts  3.33 us (2%)
    ppermute x38, waiting for transfers between devices, swap(): return lax.ppermute(value, axis, [(k, k ^ distance) for k in range(size)])  53.4 us
    pallas_call x1, Pallas kernels, expert_rows(): pl.pallas_call(functools.partial(expert_kernel, groups=groups, rows_of=ro...  42.4 us
    ppermute x38, starting transfers between devices, swap(): return lax.ppermute(value, axis, [(k, k ^ distance) for k in range(size)])  32 us
  transfers between devices with their start and end apart: 38, of which 19 were waited for; matrix products, arithmetic and copies ran while one was open for 1% of the time, Pallas kernels for 2%

profile of v1, /device:TPU:8, one launch (start us, length us, event | category | flops | bytes accessed | tf_op | source)
XLA Modules:
  0.0 139.5 jit_solution(6388099981972689446)
XLA Ops:
  0.7 0.7 copy-done.2
  1.4 0.7 copy-done.3
  2.1 2.7 %front.1 = (bf16[16,128]{1,0:T(8,128)(2,1)S(1)}, bf16[128,1024]{1,0:T(8,128)(2,1)S(1)}, bf16[384,128]{1,0:T(8,128)(2,1)S(1)}, f32[136,128]{1,0:T(8,128)S(1)}, f3...) custom-call(s32[2]{0:T(128)S(1)} %pad_add_fusion.place_ref, ...), custom_call_target="tpu_custom_call" | custom-call | tf_op jit(solution)/shard_map/front/pallas_call | solution.py:347
  4.8 1.0 collective-permute-start.2
  5.8 0.6 collective-permute-start.1
  6.9 1.4 collective-permute-start.4
  8.3 0.8 collective-permute-start.5
  9.8 1.6 %collective-permute-start.9 = (bf16[48,1152]{1,0:T(8,128)(2,1)S(1)}, bf16[48,1152]{1,0:T(8,128)(2,1)S(1)}, u32[]{:S(2)}, u32[]{:S(2)}) collective-permute-start(bf16[48,1152]{1,0:T(8,128)(2,1)S(1)} %get-tuple-element.52), channel_id=1, source_target_pairs={{0,1},{1,0},{2,3},{3,2},{4,5},{5,4},{6,7},{7,6},{8,9},{9,8},{10,11... | collective-permute-start | bytes 331784 | tf_op jit(solution)/shard_map/ppermute | solution.py:22
  11.4 0.7 dynamic_slice.6
  12.5 2.4 %collective-permute-done.9.refs_5_.refs_1_ = bf16[48,1152]{1,0:T(8,128)(2,1)S(1)} collective-permute-done((bf16[48,1152]{1,0:T(8,128)(2,1)S(1)}, bf16[48,1152]{1,0:T(8,128)(2,1)S(1)}, u32[]{:S(2)}, u32[]{:S(2)}) %collective-permute-start.9) | collective-permute-done | bytes 110624 | tf_op jit(solution)/shard_map/ppermute | solution.py:22
  14.9 1.4 %collective-permute-start.11 = (bf16[48,1152]{1,0:T(8,128)(2,1)S(1)}, bf16[48,1152]{1,0:T(8,128)(2,1)S(1)}, u32[]{:S(2)}, u32[]{:S(2)}) collective-permute-start(bf16[48,1152]{1,0:T(8,128)(2,1)S(1)} %get-tuple-element.54), channel_id=1, source_target_pairs={{0,3},{1,2},{2,1},{3,0},{4,7},{5,6},{6,5},{7,4},{8,11},{9,10},{10,... | collective-permute-start | bytes 331784 | tf_op jit(solution)/shard_map/ppermute | solution.py:22
  16.4 0.5 collective-permute-done.10.refs_6_.refs_2_
  16.9 3.7 %collective-permute-done.11.refs_7_.refs_3_ = bf16[48,1152]{1,0:T(8,128)(2,1)S(1)} collective-permute-done((bf16[48,1152]{1,0:T(8,128)(2,1)S(1)}, bf16[48,1152]{1,0:T(8,128)(2,1)S(1)}, u32[]{:S(2)}, u32[]{:S(2)}) %collective-permute-start.11) | collective-permute-done | bytes 110624 | tf_op jit(solution)/shard_map/ppermute | solution.py:22
  20.6 0.7 adapter_rows.3.refs_0_
  21.3 1.4 %collective-permute-start.17 = (bf16[192,1024]{1,0:T(8,128)(2,1)S(1)}, bf16[192,1024]{1,0:T(8,128)(2,1)S(1)}, u32[]{:S(2)}, u32[]{:S(2)}) collective-permute-start(bf16[192,1024]{1,0:T(8,128)(2,1)S(1)} %adapter_rows.3.refs_0_), channel_id=1, source_target_pairs={{0,16},{8,24},{16,0},{24,8},{1,17},{9,25},{17,1},{25,9},{2,18},{10... | collective-permute-start | bytes 1179656 | tf_op jit(solution)/shard_map/ppermute | solution.py:22
  22.7 2.6 %collective-permute-start.12 = (bf16[48,1152]{1,0:T(8,128)(2,1)S(1)}, bf16[48,1152]{1,0:T(8,128)(2,1)S(1)}, u32[]{:S(2)}, u32[]{:S(2)}) collective-permute-start(bf16[48,1152]{1,0:T(8,128)(2,1)S(1)} %get-tuple-element.55), channel_id=1, source_target_pairs={{0,4},{1,5},{2,6},{3,7},{4,0},{5,1},{6,2},{7,3},{8,12},{9,13},{10,... | collective-permute-start | bytes 331784 | tf_op jit(solution)/shard_map/ppermute | solution.py:22
  25.3 1.3 collective-permute-start.13
  26.6 1.6 %collective-permute-start.14 = (bf16[48,1152]{1,0:T(8,128)(2,1)S(1)}, bf16[48,1152]{1,0:T(8,128)(2,1)S(1)}, u32[]{:S(2)}, u32[]{:S(2)}) collective-permute-start(bf16[48,1152]{1,0:T(8,128)(2,1)S(1)} %get-tuple-element.57), channel_id=1, source_target_pairs={{0,6},{1,7},{2,4},{3,5},{4,2},{5,3},{6,0},{7,1},{8,14},{9,15},{10,... | collective-permute-start | bytes 331784 | tf_op jit(solution)/shard_map/ppermute | solution.py:22
  28.6 8.8 %collective-permute-done.12.refs_8_.refs_0_ = bf16[48,1152]{1,0:T(8,128)(2,1)S(1)} collective-permute-done((bf16[48,1152]{1,0:T(8,128)(2,1)S(1)}, bf16[48,1152]{1,0:T(8,128)(2,1)S(1)}, u32[]{:S(2)}, u32[]{:S(2)}) %collective-permute-start.12) | collective-permute-done | bytes 110624 | tf_op jit(solution)/shard_map/ppermute | solution.py:22
  37.4 2.4 %collective-permute-done.13.refs_9_.refs_1_ = bf16[48,1152]{1,0:T(8,128)(2,1)S(1)} collective-permute-done((bf16[48,1152]{1,0:T(8,128)(2,1)S(1)}, bf16[48,1152]{1,0:T(8,128)(2,1)S(1)}, u32[]{:S(2)}, u32[]{:S(2)}) %collective-permute-start.13) | collective-permute-done | bytes 110624 | tf_op jit(solution)/shard_map/ppermute | solution.py:22
  40.2 0.6 collective-permute-start.20
  40.8 1.9 %collective-permute-done.14.refs_10_.refs_0_ = bf16[48,1152]{1,0:T(8,128)(2,1)S(1)} collective-permute-done((bf16[48,1152]{1,0:T(8,128)(2,1)S(1)}, bf16[48,1152]{1,0:T(8,128)(2,1)S(1)}, u32[]{:S(2)}, u32[]{:S(2)}) %collective-permute-start.14) | collective-permute-done | bytes 110624 | tf_op jit(solution)/shard_map/ppermute | solution.py:22
  42.8 2.5 %collective-permute-done.15.refs_11_.refs_1_ = bf16[48,1152]{1,0:T(8,128)(2,1)S(1)} collective-permute-done((bf16[48,1152]{1,0:T(8,128)(2,1)S(1)}, bf16[48,1152]{1,0:T(8,128)(2,1)S(1)}, u32[]{:S(2)}, u32[]{:S(2)}) %collective-permute-start.15) | collective-permute-done | bytes 110624 | tf_op jit(solution)/shard_map/ppermute | solution.py:22
  45.7 0.6 collective-permute-start.23
  46.3 0.5 collective-permute-start.18
  47.0 0.5 collective-permute-start.21
  47.6 4.3 %collective-permute-done.23.refs_10_ = bf16[96,1024]{1,0:T(8,128)(2,1)S(1)} collective-permute-done((bf16[96,1024]{1,0:T(8,128)(2,1)S(1)}, bf16[96,1024]{1,0:T(8,128)(2,1)S(1)}, u32[]{:S(2)}, u32[]{:S(2)}) %collective-permute-start.23) | collective-permute-done | bytes 196640 | tf_op jit(solution)/shard_map/ppermute | solution.py:22
  51.9 1.4 %collective-permute-done.24.refs_11_ = bf16[96,1024]{1,0:T(8,128)(2,1)S(1)} collective-permute-done((bf16[96,1024]{1,0:T(8,128)(2,1)S(1)}, bf16[96,1024]{1,0:T(8,128)(2,1)S(1)}, u32[]{:S(2)}, u32[]{:S(2)}) %collective-permute-start.24) | collective-permute-done | bytes 196640 | tf_op jit(solution)/shard_map/ppermute | solution.py:22
  53.3 0.7 copy-done.1
  54.0 42.4 %expert_rows.1 = (bf16[2,192,1024]{2,1,0:T(8,128)(2,1)S(1)}, bf16[2,96,1024]{2,1,0:T(8,128)(2,1)S(1)}, bf16[2,96,1024]{2,1,0:T(8,128)(2,1)S(1)}, f32[2,192,1024]...) custom-call(s32[4]{0:T(128)S(1)} %iota_xor_fusion.offset_ref, f32[1,4096]{1,0:T(1,128)S(1)} %bitcast.20, ...), custom_call_target="tpu_custom_call" | custom-call | tf_op jit(solution)/shard_map/expert_rows/pallas_call | solution.py:173
  97.2 2.2 %collective-permute-done.30.other_ref = bf16[2,96,1024]{2,1,0:T(8,128)(2,1)S(1)} collective-permute-done((bf16[2,96,1024]{2,1,0:T(8,128)(2,1)S(1)}, bf16[2,96,1024]{2,1,0:T(8,128)(2,1)S(1)}, u32[]{:S(2)}, u32[]{:S(2)}) %collective-permute-start.30) | collective-permute-done | bytes 393248 | tf_op jit(solution)/shard_map/ppermute | solution.py:22
  99.4 0.5 collective-permute-start.31
  100.0 1.6 %collective-permute-start.26 = (bf16[192,1024]{1,0:T(8,128)(2,1)S(1)}, bf16[192,1024]{1,0:T(8,128)(2,1)S(1)}, u32[]{:S(2)}, u32[]{:S(2)}) collective-permute-start(bf16[192,1024]{1,0:T(8,128)(2,1)S(1)} %fusion), channel_id=1, source_target_pairs={{0,16},{8,24},{16,0},{24,8},{1,17},{9,25},{17,1},{25,9},{2,18},{10... | collective-permute-start | bytes 1179656 | tf_op jit(solution)/shard_map/ppermute | solution.py:22
  101.7 0.5 collective-permute-start.35
  102.3 5.0 %collective-permute-done.31.refs_0_ = bf16[96,1024]{1,0:T(8,128)(2,1)S(1)} collective-permute-done((bf16[96,1024]{1,0:T(8,128)(2,1)S(1)}, bf16[96,1024]{1,0:T(8,128)(2,1)S(1)}, u32[]{:S(2)}, u32[]{:S(2)}) %collective-permute-start.31) | collective-permute-done | bytes 196640 | tf_op jit(solution)/shard_map/ppermute | solution.py:22
  107.4 3.8 %collective-permute-start.32 = (bf16[48,1024]{1,0:T(8,128)(2,1)S(1)}, bf16[48,1024]{1,0:T(8,128)(2,1)S(1)}, u32[]{:S(2)}, u32[]{:S(2)}) collective-permute-start(bf16[48,1024]{1,0:T(8,128)(2,1)S(1)} %get-tuple-element.69), channel_id=1, source_target_pairs={{0,4},{1,5},{2,6},{3,7},{4,0},{5,1},{6,2},{7,3},{8,12},{9,13},{10,... | collective-permute-start | bytes 294920 | tf_op jit(solution)/shard_map/ppermute | solution.py:22
  111.2 0.7 own_rows.1
  111.9 6.5 %collective-permute-done.8.refs_3_ = f32[16,128]{1,0:T(8,128)S(1)} collective-permute-done((f32[16,128]{1,0:T(8,128)S(1)}, f32[16,128]{1,0:T(8,128)S(1)}, u32[]{:S(2)}, u32[]{:S(2)}) %collective-permute-start.8) | collective-permute-done | bytes 8224 | tf_op jit(solution)/shard_map/ppermute | solution.py:22
  118.9 3.2 %collective-permute-done.7.refs_2_ = f32[16,128]{1,0:T(8,128)S(1)} collective-permute-done((f32[16,128]{1,0:T(8,128)S(1)}, f32[16,128]{1,0:T(8,128)S(1)}, u32[]{:S(2)}, u32[]{:S(2)}) %collective-permute-start.7) | collective-permute-done | bytes 8224 | tf_op jit(solution)/shard_map/ppermute | solution.py:22
  122.1 1.2 collective-permute-done.6.refs_1_
  123.7 3.4 %collective-permute-start.36 = (bf16[48,1024]{1,0:T(8,128)(2,1)S(1)}, bf16[48,1024]{1,0:T(8,128)(2,1)S(1)}, u32[]{:S(2)}, u32[]{:S(2)}) collective-permute-start(bf16[48,1024]{1,0:T(8,128)(2,1)S(1)} %get-tuple-element.73), channel_id=1, source_target_pairs={{0,6},{1,7},{2,4},{3,5},{4,2},{5,3},{6,0},{7,1},{8,14},{9,15},{10,... | collective-permute-start | bytes 294920 | tf_op jit(solution)/shard_map/ppermute | solution.py:22
  127.3 1.6 %collective-permute-start.27 = (bf16[48,1024]{1,0:T(8,128)(2,1)S(1)}, bf16[48,1024]{1,0:T(8,128)(2,1)S(1)}, u32[]{:S(2)}, u32[]{:S(2)}) collective-permute-start(bf16[48,1024]{1,0:T(8,128)(2,1)S(1)} %get-tuple-element.64), channel_id=1, source_target_pairs={{0,1},{1,0},{2,3},{3,2},{4,5},{5,4},{6,7},{7,6},{8,9},{9,8},{10,11... | collective-permute-start | bytes 294920 | tf_op jit(solution)/shard_map/ppermute | solution.py:22
  128.9 1.8 %collective-permute-start.28 = (bf16[48,1024]{1,0:T(8,128)(2,1)S(1)}, bf16[48,1024]{1,0:T(8,128)(2,1)S(1)}, u32[]{:S(2)}, u32[]{:S(2)}) collective-permute-start(bf16[48,1024]{1,0:T(8,128)(2,1)S(1)} %get-tuple-element.65), channel_id=1, source_target_pairs={{0,2},{1,3},{2,0},{3,1},{4,6},{5,7},{6,4},{7,5},{8,10},{9,11},{10,... | collective-permute-start | bytes 294920 | tf_op jit(solution)/shard_map/ppermute | solution.py:22
  130.9 0.6 slice_bitcast_fusion
  131.4 3.5 %collective-permute-done.36.refs_6_ = bf16[48,1024]{1,0:T(8,128)(2,1)S(1)} collective-permute-done((bf16[48,1024]{1,0:T(8,128)(2,1)S(1)}, bf16[48,1024]{1,0:T(8,128)(2,1)S(1)}, u32[]{:S(2)}, u32[]{:S(2)}) %collective-permute-start.36) | collective-permute-done | bytes 98336 | tf_op jit(solution)/shard_map/ppermute | solution.py:22
  134.9 1.9 %collective-permute-done.37.refs_7_ = bf16[48,1024]{1,0:T(8,128)(2,1)S(1)} collective-permute-done((bf16[48,1024]{1,0:T(8,128)(2,1)S(1)}, bf16[48,1024]{1,0:T(8,128)(2,1)S(1)}, u32[]{:S(2)}, u32[]{:S(2)}) %collective-permute-start.37) | collective-permute-done | bytes 98336 | tf_op jit(solution)/shard_map/ppermute | solution.py:22
  136.9 1.4 %collective-permute-done.29.refs_3_ = bf16[48,1024]{1,0:T(8,128)(2,1)S(1)} collective-permute-done((bf16[48,1024]{1,0:T(8,128)(2,1)S(1)}, bf16[48,1024]{1,0:T(8,128)(2,1)S(1)}, u32[]{:S(2)}, u32[]{:S(2)}) %collective-permute-start.29) | collective-permute-done | bytes 98336 | tf_op jit(solution)/shard_map/ppermute | solution.py:22
  138.3 1.2 finish.1
  (59 shorter events, 5.6 us)
Async XLA Ops:
  0.6 110.6 %copy-start = (bf16[4096,8]{0,1:T(8,128)(2,1)S(1)}, bf16[4096,8]{0,1:T(8,128)(2,1)}, u32[]{:S(2)}) copy-start(bf16[4096,8]{0,1:T(8,128)(2,1)} %param.16) | copy-start | bytes 196612
  0.7 0.7 copy-start.2
  1.4 0.7 copy-start.3
  4.8 3.5 %collective-permute-start.2 = (bf16[16,128]{1,0:T(8,128)(2,1)S(1)}, bf16[16,128]{1,0:T(8,128)(2,1)S(1)}, u32[]{:S(2)}, u32[]{:S(2)}) collective-permute-start(bf16[16,128]{1,0:T(8,128)(2,1)S(1)} %get-tuple-element.42.refs_0_), channel_id=1, source_target_pairs={{0,24},{8,16},{16,8},{24,0},{1,25},{9,17},{17,9},{25,1},{2,26},{10... | collective-permute-start | bytes 12296 | tf_op jit(solution)/shard_map/ppermute | solution.py:22
  5.8 3.6 %collective-permute-start.1 = (bf16[16,128]{1,0:T(8,128)(2,1)S(1)}, bf16[16,128]{1,0:T(8,128)(2,1)S(1)}, u32[]{:S(2)}, u32[]{:S(2)}) collective-permute-start(bf16[16,128]{1,0:T(8,128)(2,1)S(1)} %get-tuple-element.42.refs_0_), channel_id=1, source_target_pairs={{0,16},{8,24},{16,0},{24,8},{1,17},{9,25},{17,1},{25,9},{2,18},{10... | collective-permute-start | bytes 12296 | tf_op jit(solution)/shard_map/ppermute | solution.py:22
  6.4 3.0 %collective-permute-start = (bf16[16,128]{1,0:T(8,128)(2,1)S(1)}, bf16[16,128]{1,0:T(8,128)(2,1)S(1)}, u32[]{:S(2)}, u32[]{:S(2)}) collective-permute-start(bf16[16,128]{1,0:T(8,128)(2,1)S(1)} %get-tuple-element.42.refs_0_), channel_id=1, source_target_pairs={{0,8},{8,0},{16,24},{24,16},{1,9},{9,1},{17,25},{25,17},{2,10},{10... | collective-permute-start | bytes 12296 | tf_op jit(solution)/shard_map/ppermute | solution.py:22
  6.7 13.9 %collective-permute-start.3 = (bf16[128,1024]{1,0:T(8,128)(2,1)S(1)}, bf16[128,1024]{1,0:T(8,128)(2,1)S(1)}, u32[]{:S(2)}, u32[]{:S(2)}) collective-permute-start(bf16[128,1024]{1,0:T(8,128)(2,1)S(1)} %get-tuple-element.45), channel_id=1, source_target_pairs={{0,8},{8,0},{16,24},{24,16},{1,9},{9,1},{17,25},{25,17},{2,10},{10... | collective-permute-start | bytes 786440 | tf_op jit(solution)/shard_map/ppermute | solution.py:22
  6.9 13.7 %collective-permute-start.4 = (bf16[128,1024]{1,0:T(8,128)(2,1)S(1)}, bf16[128,1024]{1,0:T(8,128)(2,1)S(1)}, u32[]{:S(2)}, u32[]{:S(2)}) collective-permute-start(bf16[128,1024]{1,0:T(8,128)(2,1)S(1)} %get-tuple-element.46), channel_id=1, source_target_pairs={{0,16},{8,24},{16,0},{24,8},{1,17},{9,25},{17,1},{25,9},{2,18},{10... | collective-permute-start | bytes 786440 | tf_op jit(solution)/shard_map/ppermute | solution.py:22
  8.3 12.3 %collective-permute-start.5 = (bf16[128,1024]{1,0:T(8,128)(2,1)S(1)}, bf16[128,1024]{1,0:T(8,128)(2,1)S(1)}, u32[]{:S(2)}, u32[]{:S(2)}) collective-permute-start(bf16[128,1024]{1,0:T(8,128)(2,1)S(1)} %get-tuple-element.47), channel_id=1, source_target_pairs={{0,24},{8,16},{16,8},{24,0},{1,25},{9,17},{17,9},{25,1},{2,26},{10... | collective-permute-start | bytes 786440 | tf_op jit(solution)/shard_map/ppermute | solution.py:22
  9.8 5.2 %collective-permute-start.9 = (bf16[48,1152]{1,0:T(8,128)(2,1)S(1)}, bf16[48,1152]{1,0:T(8,128)(2,1)S(1)}, u32[]{:S(2)}, u32[]{:S(2)}) collective-permute-start(bf16[48,1152]{1,0:T(8,128)(2,1)S(1)} %get-tuple-element.52), channel_id=1, source_target_pairs={{0,1},{1,0},{2,3},{3,2},{4,5},{5,4},{6,7},{7,6},{8,9},{9,8},{10,11... | collective-permute-start | bytes 331784 | tf_op jit(solution)/shard_map/ppermute | solution.py:22
  12.1 4.8 %collective-permute-start.10 = (bf16[48,1152]{1,0:T(8,128)(2,1)S(1)}, bf16[48,1152]{1,0:T(8,128)(2,1)S(1)}, u32[]{:S(2)}, u32[]{:S(2)}) collective-permute-start(bf16[48,1152]{1,0:T(8,128)(2,1)S(1)} %get-tuple-element.53), channel_id=1, source_target_pairs={{0,2},{1,3},{2,0},{3,1},{4,6},{5,7},{6,4},{7,5},{8,10},{9,11},{10,... | collective-permute-start | bytes 331784 | tf_op jit(solution)/shard_map/ppermute | solution.py:22
  14.9 5.6 %collective-permute-start.11 = (bf16[48,1152]{1,0:T(8,128)(2,1)S(1)}, bf16[48,1152]{1,0:T(8,128)(2,1)S(1)}, u32[]{:S(2)}, u32[]{:S(2)}) collective-permute-start(bf16[48,1152]{1,0:T(8,128)(2,1)S(1)} %get-tuple-element.54), channel_id=1, source_target_pairs={{0,3},{1,2},{2,1},{3,0},{4,7},{5,6},{6,5},{7,4},{8,11},{9,10},{10,... | collective-permute-start | bytes 331784 | tf_op jit(solution)/shard_map/ppermute | solution.py:22
  21.3 25.0 %collective-permute-start.17 = (bf16[192,1024]{1,0:T(8,128)(2,1)S(1)}, bf16[192,1024]{1,0:T(8,128)(2,1)S(1)}, u32[]{:S(2)}, u32[]{:S(2)}) collective-permute-start(bf16[192,1024]{1,0:T(8,128)(2,1)S(1)} %adapter_rows.3.refs_0_), channel_id=1, source_target_pairs={{0,16},{8,24},{16,0},{24,8},{1,17},{9,25},{17,1},{25,9},{2,18},{10... | collective-permute-start | bytes 1179656 | tf_op jit(solution)/shard_map/ppermute | solution.py:22
  22.7 14.6 %collective-permute-start.12 = (bf16[48,1152]{1,0:T(8,128)(2,1)S(1)}, bf16[48,1152]{1,0:T(8,128)(2,1)S(1)}, u32[]{:S(2)}, u32[]{:S(2)}) collective-permute-start(bf16[48,1152]{1,0:T(8,128)(2,1)S(1)} %get-tuple-element.55), channel_id=1, source_target_pairs={{0,4},{1,5},{2,6},{3,7},{4,0},{5,1},{6,2},{7,3},{8,12},{9,13},{10,... | collective-permute-start | bytes 331784 | tf_op jit(solution)/shard_map/ppermute | solution.py:22
  25.3 14.4 %collective-permute-start.13 = (bf16[48,1152]{1,0:T(8,128)(2,1)S(1)}, bf16[48,1152]{1,0:T(8,128)(2,1)S(1)}, u32[]{:S(2)}, u32[]{:S(2)}) collective-permute-start(bf16[48,1152]{1,0:T(8,128)(2,1)S(1)} %get-tuple-element.56), channel_id=1, source_target_pairs={{0,5},{1,4},{2,7},{3,6},{4,1},{5,0},{6,3},{7,2},{8,13},{9,12},{10,... | collective-permute-start | bytes 331784 | tf_op jit(solution)/shard_map/ppermute | solution.py:22
  26.6 16.2 %collective-permute-start.14 = (bf16[48,1152]{1,0:T(8,128)(2,1)S(1)}, bf16[48,1152]{1,0:T(8,128)(2,1)S(1)}, u32[]{:S(2)}, u32[]{:S(2)}) collective-permute-start(bf16[48,1152]{1,0:T(8,128)(2,1)S(1)} %get-tuple-element.57), channel_id=1, source_target_pairs={{0,6},{1,7},{2,4},{3,5},{4,2},{5,3},{6,0},{7,1},{8,14},{9,15},{10,... | collective-permute-start | bytes 331784 | tf_op jit(solution)/shard_map/ppermute | solution.py:22
  28.2 17.1 %collective-permute-start.15 = (bf16[48,1152]{1,0:T(8,128)(2,1)S(1)}, bf16[48,1152]{1,0:T(8,128)(2,1)S(1)}, u32[]{:S(2)}, u32[]{:S(2)}) collective-permute-start(bf16[48,1152]{1,0:T(8,128)(2,1)S(1)} %get-tuple-element.58), channel_id=1, source_target_pairs={{0,7},{1,6},{2,5},{3,4},{4,3},{5,2},{6,1},{7,0},{8,15},{9,14},{10,... | collective-permute-start | bytes 331784 | tf_op jit(solution)/shard_map/ppermute | solution.py:22
  40.2 6.8 %collective-permute-start.20 = (bf16[96,1024]{1,0:T(8,128)(2,1)S(1)}, bf16[96,1024]{1,0:T(8,128)(2,1)S(1)}, u32[]{:S(2)}, u32[]{:S(2)}) collective-permute-start(bf16[96,1024]{1,0:T(8,128)(2,1)S(1)} %adapter_rows.4.refs_4_), channel_id=1, source_target_pairs={{0,16},{8,24},{16,0},{24,8},{1,17},{9,25},{17,1},{25,9},{2,18},{10... | collective-permute-start | bytes 589832 | tf_op jit(solution)/shard_map/ppermute | solution.py:22
  40.8 6.2 %collective-permute-start.19 = (bf16[96,1024]{1,0:T(8,128)(2,1)S(1)}, bf16[96,1024]{1,0:T(8,128)(2,1)S(1)}, u32[]{:S(2)}, u32[]{:S(2)}) collective-permute-start(bf16[96,1024]{1,0:T(8,128)(2,1)S(1)} %adapter_rows.4.refs_4_), channel_id=1, source_target_pairs={{0,8},{8,0},{16,24},{24,16},{1,9},{9,1},{17,25},{25,17},{2,10},{10... | collective-permute-start | bytes 589832 | tf_op jit(solution)/shard_map/ppermute | solution.py:22
  45.7 6.1 %collective-permute-start.23 = (bf16[96,1024]{1,0:T(8,128)(2,1)S(1)}, bf16[96,1024]{1,0:T(8,128)(2,1)S(1)}, u32[]{:S(2)}, u32[]{:S(2)}) collective-permute-start(bf16[96,1024]{1,0:T(8,128)(2,1)S(1)} %adapter_rows.5.refs_8_), channel_id=1, source_target_pairs={{0,16},{8,24},{16,0},{24,8},{1,17},{9,25},{17,1},{25,9},{2,18},{10... | collective-permute-start | bytes 589832 | tf_op jit(solution)/shard_map/ppermute | solution.py:22
  46.3 7.0 %collective-permute-start.16 = (bf16[192,1024]{1,0:T(8,128)(2,1)S(1)}, bf16[192,1024]{1,0:T(8,128)(2,1)S(1)}, u32[]{:S(2)}, u32[]{:S(2)}) collective-permute-start(bf16[192,1024]{1,0:T(8,128)(2,1)S(1)} %adapter_rows.3.refs_0_), channel_id=1, source_target_pairs={{0,8},{8,0},{16,24},{24,16},{1,9},{9,1},{17,25},{25,17},{2,10},{10... | collective-permute-start | bytes 1179656 | tf_op jit(solution)/shard_map/ppermute | solution.py:22
  46.3 7.0 %collective-permute-start.18 = (bf16[192,1024]{1,0:T(8,128)(2,1)S(1)}, bf16[192,1024]{1,0:T(8,128)(2,1)S(1)}, u32[]{:S(2)}, u32[]{:S(2)}) collective-permute-start(bf16[192,1024]{1,0:T(8,128)(2,1)S(1)} %collective-permute-done.17.refs_2_), channel_id=1, source_target_pairs={{0,8},{8,0},{16,24},{24,16},{1,9},{9,1},{17,25},{25,17},{2,10},{10... | collective-permute-start | bytes 1179656 | tf_op jit(solution)/shard_map/ppermute | solution.py:22
  47.0 4.8 %collective-permute-start.22 = (bf16[96,1024]{1,0:T(8,128)(2,1)S(1)}, bf16[96,1024]{1,0:T(8,128)(2,1)S(1)}, u32[]{:S(2)}, u32[]{:S(2)}) collective-permute-start(bf16[96,1024]{1,0:T(8,128)(2,1)S(1)} %adapter_rows.5.refs_8_), channel_id=1, source_target_pairs={{0,8},{8,0},{16,24},{24,16},{1,9},{9,1},{17,25},{25,17},{2,10},{10... | collective-permute-start | bytes 589832 | tf_op jit(solution)/shard_map/ppermute | solution.py:22
  47.0 4.8 %collective-permute-start.21 = (bf16[96,1024]{1,0:T(8,128)(2,1)S(1)}, bf16[96,1024]{1,0:T(8,128)(2,1)S(1)}, u32[]{:S(2)}, u32[]{:S(2)}) collective-permute-start(bf16[96,1024]{1,0:T(8,128)(2,1)S(1)} %collective-permute-done.20.refs_6_), channel_id=1, source_target_pairs={{0,8},{8,0},{16,24},{24,16},{1,9},{9,1},{17,25},{25,17},{2,10},{10... | collective-permute-start | bytes 589832 | tf_op jit(solution)/shard_map/ppermute | solution.py:22
  51.9 1.4 %collective-permute-start.24 = (bf16[96,1024]{1,0:T(8,128)(2,1)S(1)}, bf16[96,1024]{1,0:T(8,128)(2,1)S(1)}, u32[]{:S(2)}, u32[]{:S(2)}) collective-permute-start(bf16[96,1024]{1,0:T(8,128)(2,1)S(1)} %collective-permute-done.23.refs_10_), channel_id=1, source_target_pairs={{0,8},{8,0},{16,24},{24,16},{1,9},{9,1},{17,25},{25,17},{2,10},{10... | collective-permute-start | bytes 589832 | tf_op jit(solution)/shard_map/ppermute | solution.py:22
  53.3 0.7 copy-start.1
  96.5 3.5 %collective-permute-start.25 = (bf16[2,192,1024]{2,1,0:T(8,128)(2,1)S(1)}, bf16[2,192,1024]{2,1,0:T(8,128)(2,1)S(1)}, u32[]{:S(2)}, u32[]{:S(2)}) collective-permute-start(bf16[2,192,1024]{2,1,0:T(8,128)(2,1)S(1)} %get-tuple-element.62), channel_id=1, source_target_pairs={{0,8},{8,0},{16,24},{24,16},{1,9},{9,1},{17,25},{25,17},{2,10},{10... | collective-permute-start | bytes 2359304 | tf_op jit(solution)/shard_map/ppermute | solution.py:22
  96.7 2.7 %collective-permute-start.30 = (bf16[2,96,1024]{2,1,0:T(8,128)(2,1)S(1)}, bf16[2,96,1024]{2,1,0:T(8,128)(2,1)S(1)}, u32[]{:S(2)}, u32[]{:S(2)}) collective-permute-start(bf16[2,96,1024]{2,1,0:T(8,128)(2,1)S(1)} %get-tuple-element.68), channel_id=1, source_target_pairs={{0,8},{8,0},{16,24},{24,16},{1,9},{9,1},{17,25},{25,17},{2,10},{10... | collective-permute-start | bytes 1179656 | tf_op jit(solution)/shard_map/ppermute | solution.py:22
  97.0 4.6 %collective-permute-start.34 = (bf16[2,96,1024]{2,1,0:T(8,128)(2,1)S(1)}, bf16[2,96,1024]{2,1,0:T(8,128)(2,1)S(1)}, u32[]{:S(2)}, u32[]{:S(2)}) collective-permute-start(bf16[2,96,1024]{2,1,0:T(8,128)(2,1)S(1)} %get-tuple-element.72), channel_id=1, source_target_pairs={{0,8},{8,0},{16,24},{24,16},{1,9},{9,1},{17,25},{25,17},{2,10},{10... | collective-permute-start | bytes 1179656 | tf_op jit(solution)/shard_map/ppermute | solution.py:22
  99.4 7.8 %collective-permute-start.31 = (bf16[96,1024]{1,0:T(8,128)(2,1)S(1)}, bf16[96,1024]{1,0:T(8,128)(2,1)S(1)}, u32[]{:S(2)}, u32[]{:S(2)}) collective-permute-start(bf16[96,1024]{1,0:T(8,128)(2,1)S(1)} %fusion.1), channel_id=1, source_target_pairs={{0,16},{8,24},{16,0},{24,8},{1,17},{9,25},{17,1},{25,9},{2,18},{10... | collective-permute-start | bytes 589832 | tf_op jit(solution)/shard_map/ppermute | solution.py:22
  100.0 27.1 %collective-permute-start.26 = (bf16[192,1024]{1,0:T(8,128)(2,1)S(1)}, bf16[192,1024]{1,0:T(8,128)(2,1)S(1)}, u32[]{:S(2)}, u32[]{:S(2)}) collective-permute-start(bf16[192,1024]{1,0:T(8,128)(2,1)S(1)} %fusion), channel_id=1, source_target_pairs={{0,16},{8,24},{16,0},{24,8},{1,17},{9,25},{17,1},{25,9},{2,18},{10... | collective-permute-start | bytes 1179656 | tf_op jit(solution)/shard_map/ppermute | solution.py:22
  101.7 21.9 %collective-permute-start.35 = (bf16[96,1024]{1,0:T(8,128)(2,1)S(1)}, bf16[96,1024]{1,0:T(8,128)(2,1)S(1)}, u32[]{:S(2)}, u32[]{:S(2)}) collective-permute-start(bf16[96,1024]{1,0:T(8,128)(2,1)S(1)} %fusion.2), channel_id=1, source_target_pairs={{0,16},{8,24},{16,0},{24,8},{1,17},{9,25},{17,1},{25,9},{2,18},{10... | collective-permute-start | bytes 589832 | tf_op jit(solution)/shard_map/ppermute | solution.py:22
  107.4 21.5 %collective-permute-start.32 = (bf16[48,1024]{1,0:T(8,128)(2,1)S(1)}, bf16[48,1024]{1,0:T(8,128)(2,1)S(1)}, u32[]{:S(2)}, u32[]{:S(2)}) collective-permute-start(bf16[48,1024]{1,0:T(8,128)(2,1)S(1)} %get-tuple-element.69), channel_id=1, source_target_pairs={{0,4},{1,5},{2,6},{3,7},{4,0},{5,1},{6,2},{7,3},{8,12},{9,13},{10,... | collective-permute-start | bytes 294920 | tf_op jit(solution)/shard_map/ppermute | solution.py:22
  111.1 19.6 %collective-permute-start.33 = (bf16[48,1024]{1,0:T(8,128)(2,1)S(1)}, bf16[48,1024]{1,0:T(8,128)(2,1)S(1)}, u32[]{:S(2)}, u32[]{:S(2)}) collective-permute-start(bf16[48,1024]{1,0:T(8,128)(2,1)S(1)} %get-tuple-element.70), channel_id=1, source_target_pairs={{0,5},{1,4},{2,7},{3,6},{4,1},{5,0},{6,3},{7,2},{8,13},{9,12},{10,... | collective-permute-start | bytes 294920 | tf_op jit(solution)/shard_map/ppermute | solution.py:22
  111.9 6.5 %collective-permute-start.8 = (f32[16,128]{1,0:T(8,128)S(1)}, f32[16,128]{1,0:T(8,128)S(1)}, u32[]{:S(2)}, u32[]{:S(2)}) collective-permute-start(f32[16,128]{1,0:T(8,128)S(1)} %get-tuple-element.50.refs_0_), channel_id=1, source_target_pairs={{0,24},{8,16},{16,8},{24,0},{1,25},{9,17},{17,9},{25,1},{2,26},{10... | collective-permute-start | bytes 24584 | tf_op jit(solution)/shard_map/ppermute | solution.py:22
  118.4 3.7 %collective-permute-start.7 = (f32[16,128]{1,0:T(8,128)S(1)}, f32[16,128]{1,0:T(8,128)S(1)}, u32[]{:S(2)}, u32[]{:S(2)}) collective-permute-start(f32[16,128]{1,0:T(8,128)S(1)} %get-tuple-element.50.refs_0_), channel_id=1, source_target_pairs={{0,16},{8,24},{16,0},{24,8},{1,17},{9,25},{17,1},{25,9},{2,18},{10... | collective-permute-start | bytes 24584 | tf_op jit(solution)/shard_map/ppermute | solution.py:22
  122.1 1.2 collective-permute-start.6
  123.7 11.2 %collective-permute-start.36 = (bf16[48,1024]{1,0:T(8,128)(2,1)S(1)}, bf16[48,1024]{1,0:T(8,128)(2,1)S(1)}, u32[]{:S(2)}, u32[]{:S(2)}) collective-permute-start(bf16[48,1024]{1,0:T(8,128)(2,1)S(1)} %get-tuple-element.73), channel_id=1, source_target_pairs={{0,6},{1,7},{2,4},{3,5},{4,2},{5,3},{6,0},{7,1},{8,14},{9,15},{10,... | collective-permute-start | bytes 294920 | tf_op jit(solution)/shard_map/ppermute | solution.py:22
  127.1 9.7 %collective-permute-start.37 = (bf16[48,1024]{1,0:T(8,128)(2,1)S(1)}, bf16[48,1024]{1,0:T(8,128)(2,1)S(1)}, u32[]{:S(2)}, u32[]{:S(2)}) collective-permute-start(bf16[48,1024]{1,0:T(8,128)(2,1)S(1)} %get-tuple-element.74), channel_id=1, source_target_pairs={{0,7},{1,6},{2,5},{3,4},{4,3},{5,2},{6,1},{7,0},{8,15},{9,14},{10,... | collective-permute-start | bytes 294920 | tf_op jit(solution)/shard_map/ppermute | solution.py:22
  127.3 9.6 %collective-permute-start.27 = (bf16[48,1024]{1,0:T(8,128)(2,1)S(1)}, bf16[48,1024]{1,0:T(8,128)(2,1)S(1)}, u32[]{:S(2)}, u32[]{:S(2)}) collective-permute-start(bf16[48,1024]{1,0:T(8,128)(2,1)S(1)} %get-tuple-element.64), channel_id=1, source_target_pairs={{0,1},{1,0},{2,3},{3,2},{4,5},{5,4},{6,7},{7,6},{8,9},{9,8},{10,11... | collective-permute-start | bytes 294920 | tf_op jit(solution)/shard_map/ppermute | solution.py:22
  128.9 8.0 %collective-permute-start.28 = (bf16[48,1024]{1,0:T(8,128)(2,1)S(1)}, bf16[48,1024]{1,0:T(8,128)(2,1)S(1)}, u32[]{:S(2)}, u32[]{:S(2)}) collective-permute-start(bf16[48,1024]{1,0:T(8,128)(2,1)S(1)} %get-tuple-element.65), channel_id=1, source_target_pairs={{0,2},{1,3},{2,0},{3,1},{4,6},{5,7},{6,4},{7,5},{8,10},{9,11},{10,... | collective-permute-start | bytes 294920 | tf_op jit(solution)/shard_map/ppermute | solution.py:22
  130.7 7.6 %collective-permute-start.29 = (bf16[48,1024]{1,0:T(8,128)(2,1)S(1)}, bf16[48,1024]{1,0:T(8,128)(2,1)S(1)}, u32[]{:S(2)}, u32[]{:S(2)}) collective-permute-start(bf16[48,1024]{1,0:T(8,128)(2,1)S(1)} %get-tuple-element.66), channel_id=1, source_target_pairs={{0,3},{1,2},{2,1},{3,0},{4,7},{5,6},{6,5},{7,4},{8,11},{9,10},{10,... | collective-permute-start | bytes 294920 | tf_op jit(solution)/shard_map/ppermute | solution.py:22

commit v2 on v1

--- a/solution.py
+++ b/solution.py
@@ -29,14 +29,14 @@
     return tile
 
 
-def expert_kernel(offset_ref, gain_hbm, *refs, groups, rows_of, owners):
+def expert_kernel(offset_ref, inverse_ref, *refs, groups, rows_of, owners):
     count = len(rows_of)
     number_of_groups = len(groups)
     pieces, refs = refs[:count], refs[count:]
     gate_ref, up_ref, down_ref = refs[:3]
     send_refs = refs[3 : 3 + number_of_groups]
     keep_refs = refs[3 + number_of_groups : 3 + 2 * number_of_groups]
-    x_ref, hidden_ref, inv_ref, gain_ref, ring_ref, piece_sem, ring_sem = refs[
+    x_ref, hidden_ref, inv_ref, ring_ref, piece_sem, ring_sem = refs[
         3 + 2 * number_of_groups :
     ]
     total_rows, model_width = x_ref.shape
@@ -72,7 +72,7 @@
             ring_sem.at[slot],
         )
 
-    copies = [pltpu.make_async_copy(gain_hbm, gain_ref, piece_sem.at[count])]
+    copies = []
     for number, piece in enumerate(pieces):
         first, index = rows_of[number]
         start = pl.multiple_of(offset_ref[index] * width, LANES)
@@ -83,24 +83,28 @@
                 piece_sem.at[number],
             )
         )
-    for copy in copies:
-        copy.start()
-    for n in range(ahead):
+
+    def fetch(n):
         if n < pairs:
             gate_copy(n).start()
             up_copy(n).start()
         else:
             down_copy(2 * (n - pairs)).start()
             down_copy(2 * (n - pairs) + 1).start()
+
+    fetch(0)
+    for copy in copies:
+        copy.start()
+    for n in range(1, ahead):
+        fetch(n)
     for copy in copies:
         copy.wait()
 
     chunk = 16
-    gain_ref[...] = 1.0 / gain_ref[...]
 
     def norm_step(c, carry):
         rows = pl.ds(pl.multiple_of(c * chunk, chunk), chunk)
-        values = x_ref[rows, :].astype(jnp.float32) * gain_ref[...]
+        values = x_ref[rows, :].astype(jnp.float32) * inverse_ref[...]
         mean = jnp.sum(values * values, axis=1, keepdims=True) / model_width
         inv_ref[rows, :] = jnp.broadcast_to(lax.rsqrt(mean + EPS), (chunk, LANES))
         return carry
@@ -161,7 +165,7 @@
     phase(sends, keep_refs)
 
 
-def expert_rows(pieces, rows_of, groups, offsets, gain, gate_weight, up_weight, down_weight):
+def expert_rows(pieces, rows_of, groups, offsets, inverse, gate_weight, up_weight, down_weight):
     model_width, hidden_width = gate_weight.shape[1:]
     owners = offsets.shape[0]
     width = model_width // owners
@@ -174,7 +178,7 @@
         functools.partial(expert_kernel, groups=groups, rows_of=rows_of, owners=owners),
         out_shape=[jax.ShapeDtypeStruct((owners // 2, rows, width), bf16) for _, rows in groups]
         + [jax.ShapeDtypeStruct((owners // 2, rows, width), f32) for _, rows in groups],
-        in_specs=[pl.BlockSpec(memory_space=pltpu.SMEM), pl.BlockSpec(memory_space=pltpu.HBM)]
+        in_specs=[pl.BlockSpec(memory_space=pltpu.SMEM), pl.BlockSpec(memory_space=pltpu.VMEM)]
         + [pl.BlockSpec(memory_space=pl.ANY)] * len(pieces)
         + [pl.BlockSpec(memory_space=pltpu.HBM)] * 3,
         out_specs=[pl.BlockSpec(memory_space=pltpu.VMEM)] * (2 * len(groups)),
@@ -182,14 +186,13 @@
             pltpu.VMEM((total_rows, model_width), bf16),
             pltpu.VMEM((total_rows, hidden_width), bf16),
             pltpu.VMEM((total_rows, LANES), f32),
-            pltpu.VMEM((1, model_width), f32),
             pltpu.VMEM((RING, model_width, tile), bf16),
-            pltpu.SemaphoreType.DMA((len(pieces) + 1,)),
+            pltpu.SemaphoreType.DMA((len(pieces),)),
             pltpu.SemaphoreType.DMA((RING,)),
         ],
         compiler_params=pltpu.CompilerParams(vmem_limit_bytes=45 << 20),
         name="expert_rows",
-    )(offsets, gain, *pieces, gate_weight, up_weight, down_weight)
+    )(offsets, inverse, *pieces, gate_weight, up_weight, down_weight)
 
 
 def with_adapter(rows, up_refs, spread_ref, adapter_ref, width):
@@ -262,11 +265,20 @@
 
 
 def front_kernel(
-    place_ref, ids_ref, experts_ref, head_hbm, down_hbm, up_ref, stream_ref, *refs, owners, sizes
+    place_ref,
+    table_ref,
+    head_hbm,
+    down_hbm,
+    up_ref,
+    stream_ref,
+    *refs,
+    owners,
+    sizes,
 ):
     low_ref, stream_out, pick_ref, extra_ref, target_ref = refs[:5]
     up_outs = refs[5:-3]
     head_ref, down_ref, sem = refs[-3:]
+    experts_ref, ids_ref = table_ref.at[0:2], table_ref.at[2:3]
     width = stream_out.shape[1]
     held_width = down_ref.shape[1]
     owner = place_ref[0]
@@ -338,7 +350,7 @@
         copy.wait()
 
 
-def front(place, head_outputs, down_factors, ids, experts_of, up_factors, stream, owners, sizes):
+def front(place, table, head_outputs, down_factors, up_factors, stream, owners, sizes):
     rows, model_width = head_outputs.shape
     total_rows = sizes[0] * sizes[1] * CAP
     width = model_width // owners
@@ -354,7 +366,7 @@
             jax.ShapeDtypeStruct((rows, LANES), jnp.float32),
         ]
         + [jax.ShapeDtypeStruct((up_factors.shape[0], width), bf16)] * owners,
-        in_specs=[pl.BlockSpec(memory_space=pltpu.SMEM), vmem, vmem] + [hbm] * 4,
+        in_specs=[pl.BlockSpec(memory_space=pltpu.SMEM), vmem] + [hbm] * 4,
         out_specs=[vmem] * (5 + owners),
         scratch_shapes=[
             pltpu.VMEM(head_outputs.shape, bf16),
@@ -363,7 +375,7 @@
         ],
         compiler_params=pltpu.CompilerParams(vmem_limit_bytes=52 << 20),
         name="front",
-    )(place, ids[None, :], experts_of.T, head_outputs, down_factors, up_factors, stream)
+    )(place, table, head_outputs, down_factors, up_factors, stream)
 
 
 def route_kernel(pick_ref, extra_ref, stream_ref, *refs, owners):
@@ -402,8 +414,10 @@
 
 
 def own_kernel(payload_ref, *refs):
-    up_refs = refs[:-6]
-    spread_ref, adapter_ref, gain_ref, router_ref, residual_ref, stats_ref = refs[-6:]
+    up_refs = refs[:-8]
+    spread_ref, adapter_ref, gain_ref, router_ref, gains_ref = refs[-8:-3]
+    residual_ref, stats_ref, inverse_ref = refs[-3:]
+    inverse_ref[...] = 1.0 / gains_ref[...]
     rows = payload_ref[...]
     total = with_adapter(rows, up_refs, spread_ref, adapter_ref, gain_ref.shape[1])
     residual_ref[...] = total
@@ -418,17 +432,18 @@
     stats_ref[experts : 2 * experts, :] = squares[:experts]
 
 
-def own_rows(payload, up_parts, spread, adapter_of, gain, router):
+def own_rows(payload, up_parts, spread, adapter_of, gain, router, gains):
     tokens, width = payload.shape[0], gain.shape[1]
     return pl.pallas_call(
         own_kernel,
         out_shape=[
             jax.ShapeDtypeStruct((tokens, width), jnp.float32),
             jax.ShapeDtypeStruct((2 * router.shape[0], tokens), jnp.float32),
+            jax.ShapeDtypeStruct(gains.shape, jnp.float32),
         ],
         compiler_params=pltpu.CompilerParams(vmem_limit_bytes=16 << 20),
         name="own_rows",
-    )(payload, *up_parts, spread, adapter_of, gain, router)
+    )(payload, *up_parts, spread, adapter_of, gain, router, gains)
 
 
 def mix_kernel(target_ref, *refs, blocks, halves, model_width):
@@ -456,10 +471,12 @@
     high = mixing.astype(jnp.bfloat16)
     high_ref[...] = high
     rest_ref[...] = (mixing - high.astype(f32)).astype(jnp.bfloat16)
-    load_ref[...] = sum(ref[...].astype(f32)[:1, :] for ref in block_refs)
-
-
-def mix(targets, stats, blocks, experts, model_width):
+    load = sum(ref[...].astype(f32)[:1, :] for ref in block_refs)
+    first = 2 * ADAPTER_RANK
+    load_ref[...] = load[:, first : first + load_ref.shape[1]]
+
+
+def mix(targets, stats, blocks, experts, model_width, held_count):
     tokens = targets.shape[0]
     peers = len(blocks)
     width = blocks[0].shape[1] - LANES
@@ -472,11 +489,11 @@
         ),
         grid=(1,),
         out_shape=[jax.ShapeDtypeStruct((tokens, total_rows), jnp.bfloat16)] * 2
-        + [jax.ShapeDtypeStruct((1, LANES), jnp.float32)],
+        + [jax.ShapeDtypeStruct((1, held_count), jnp.float32)],
         in_specs=[full(targets.shape)]
         + [full(stat.shape) for stat in stats]
         + [corner] * peers,
-        out_specs=[full((tokens, total_rows))] * 2 + [full((1, LANES))],
+        out_specs=[full((tokens, total_rows))] * 2 + [full((1, held_count))],
         compiler_params=pltpu.CompilerParams(vmem_limit_bytes=16 << 20),
         name="mix",
     )(targets, *stats, *blocks)
@@ -526,10 +543,9 @@
     place = jnp.stack([index_aa, index_ba])
     low, stream_share, pick, extra, targets, *up_parts = front(
         place,
+        jnp.concatenate([token_expert_index.T, token_adapter_index[None, :]], axis=0),
         head_outputs,
         adapter_down_factors,
-        token_adapter_index,
-        token_expert_index,
         adapter_up_factors,
         stream,
         owners,
@@ -563,10 +579,14 @@
             rows_of += [(first * CAP, 2 * number), (first * CAP, 2 * number + 1)]
 
     router = lax.dynamic_slice_in_dim(router_matrix.T, index_aa * width, width, 1)
-    residual_share, stats = own_rows(payload, up_parts, spread, adapter_of, gain, router)
+    residual_share, stats, inverse = own_rows(
+        payload, up_parts, spread, adapter_of, gain, router, norm_gain_vector[None, :]
+    )
     stats = [stats] + [swap(stats, "aa", r) for r in range(1, owners)]
-    high, rest, load = mix(targets, stats, received, experts, model_width)
-    adapter_load = load[0, 2 * ADAPTER_RANK : 2 * ADAPTER_RANK + held_count]
+    high, rest, load = mix(
+        targets, stats, received, experts, model_width, held_count
+    )
+    adapter_load = load.reshape(held_count)
 
     offsets = index_aa ^ jnp.arange(owners, dtype=i32)
     results = expert_rows(
@@ -574,7 +594,7 @@
         tuple(rows_of),
         tuple(groups),
         offsets,
-        norm_gain_vector[None, :],
+        inverse,
         gate_weight,
         up_weight,
         down_weight,

time: 142 us -> 137 us (0.965)
  waiting for transfers between devices: 53.4 us -> 46.7 us
  starting transfers between devices: 32 us -> 35.1 us
  local copies, waits for them, and re-layouts: 3.33 us -> 1.42 us
    ppermute x38, waiting for transfers between devices: 53.4 us -> 46.7 us  [swap(): return lax.ppermute(value, axis, [(k, k ^ distance) for k in range(size)])]
    ppermute x38, starting transfers between devices: 32 us -> 35.1 us  [swap(): return lax.ppermute(value, axis, [(k, k ^ distance) for k in range(size)])]
  transfers between devices with their start and end apart: 38 -> 38, of which waited for: 19 -> 17; matrix products, arithmetic and copies ran while one was open for 1% -> 1% of each run, Pallas kernels for 2% -> 2%
where the time goes in v2:
time: 137 us; the launch traced here: 135 us
  Pallas kernels  50 us (36%)
  waiting for transfers between devices  46.7 us (34%)
  starting transfers between devices  35.1 us (26%)
  local copies, waits for them, and re-layouts  1.42 us (1%)
    ppermute x38, waiting for transfers between devices, swap(): return lax.ppermute(value, axis, [(k, k ^ distance) for k in range(size)])  46.7 us
    pallas_call x1, Pallas kernels, expert_rows(): pl.pallas_call(functools.partial(expert_kernel, groups=groups, rows_of=ro...  42.3 us
    ppermute x38, starting transfers between devices, swap(): return lax.ppermute(value, axis, [(k, k ^ distance) for k in range(size)])  35.1 us
  transfers between devices with their start and end apart: 38, of which 17 were waited for; matrix products, arithmetic and copies ran while one was open for 1% of the time, Pallas kernels for 2%

profile of v2, /device:TPU:8, one launch (start us, length us, event | category | flops | bytes accessed | tf_op | source)
XLA Modules:
  0.0 135.1 jit_solution(10180580042720592205)
XLA Ops:
  0.7 0.7 pad_add_fusion.table_ref
  1.4 2.7 %front.1 = (bf16[16,128]{1,0:T(8,128)(2,1)S(1)}, bf16[128,1024]{1,0:T(8,128)(2,1)S(1)}, bf16[384,128]{1,0:T(8,128)(2,1)S(1)}, f32[136,128]{1,0:T(8,128)S(1)}, f3...) custom-call(s32[2]{0:T(128)S(1)} %pad_add_fusion.1.place_ref, ...), custom_call_target="tpu_custom_call" | custom-call | tf_op jit(solution)/shard_map/front/pallas_call | solution.py:359
  4.2 1.0 collective-permute-start.2
  5.1 0.6 collective-permute-start.1
  6.3 1.4 %collective-permute-start.4 = (bf16[128,1024]{1,0:T(8,128)(2,1)S(1)}, bf16[128,1024]{1,0:T(8,128)(2,1)S(1)}, u32[]{:S(2)}, u32[]{:S(2)}) collective-permute-start(bf16[128,1024]{1,0:T(8,128)(2,1)S(1)} %get-tuple-element.47), channel_id=1, source_target_pairs={{0,16},{8,24},{16,0},{24,8},{1,17},{9,25},{17,1},{25,9},{2,18},{10... | collective-permute-start | bytes 786440 | tf_op jit(solution)/shard_map/ppermute | solution.py:22
  7.7 0.8 collective-permute-start.5
  9.2 1.6 %collective-permute-start.9 = (bf16[48,1152]{1,0:T(8,128)(2,1)S(1)}, bf16[48,1152]{1,0:T(8,128)(2,1)S(1)}, u32[]{:S(2)}, u32[]{:S(2)}) collective-permute-start(bf16[48,1152]{1,0:T(8,128)(2,1)S(1)} %get-tuple-element.53), channel_id=1, source_target_pairs={{0,1},{1,0},{2,3},{3,2},{4,5},{5,4},{6,7},{7,6},{8,9},{9,8},{10,11... | collective-permute-start | bytes 331784 | tf_op jit(solution)/shard_map/ppermute | solution.py:22
  10.7 0.7 dynamic_slice.6
  11.9 2.4 %collective-permute-done.9.refs_5_.refs_1_ = bf16[48,1152]{1,0:T(8,128)(2,1)S(1)} collective-permute-done((bf16[48,1152]{1,0:T(8,128)(2,1)S(1)}, bf16[48,1152]{1,0:T(8,128)(2,1)S(1)}, u32[]{:S(2)}, u32[]{:S(2)}) %collective-permute-start.9) | collective-permute-done | bytes 110624 | tf_op jit(solution)/shard_map/ppermute | solution.py:22
  14.3 1.4 %collective-permute-start.11 = (bf16[48,1152]{1,0:T(8,128)(2,1)S(1)}, bf16[48,1152]{1,0:T(8,128)(2,1)S(1)}, u32[]{:S(2)}, u32[]{:S(2)}) collective-permute-start(bf16[48,1152]{1,0:T(8,128)(2,1)S(1)} %get-tuple-element.55), channel_id=1, source_target_pairs={{0,3},{1,2},{2,1},{3,0},{4,7},{5,6},{6,5},{7,4},{8,11},{9,10},{10,... | collective-permute-start | bytes 331784 | tf_op jit(solution)/shard_map/ppermute | solution.py:22
  15.7 0.5 collective-permute-done.10.refs_6_.refs_2_
  16.2 3.7 %collective-permute-done.11.refs_7_.refs_3_ = bf16[48,1152]{1,0:T(8,128)(2,1)S(1)} collective-permute-done((bf16[48,1152]{1,0:T(8,128)(2,1)S(1)}, bf16[48,1152]{1,0:T(8,128)(2,1)S(1)}, u32[]{:S(2)}, u32[]{:S(2)}) %collective-permute-start.11) | collective-permute-done | bytes 110624 | tf_op jit(solution)/shard_map/ppermute | solution.py:22
  20.0 0.7 adapter_rows.3.refs_0_
  20.7 1.4 %collective-permute-start.17 = (bf16[192,1024]{1,0:T(8,128)(2,1)S(1)}, bf16[192,1024]{1,0:T(8,128)(2,1)S(1)}, u32[]{:S(2)}, u32[]{:S(2)}) collective-permute-start(bf16[192,1024]{1,0:T(8,128)(2,1)S(1)} %adapter_rows.3.refs_0_), channel_id=1, source_target_pairs={{0,16},{8,24},{16,0},{24,8},{1,17},{9,25},{17,1},{25,9},{2,18},{10... | collective-permute-start | bytes 1179656 | tf_op jit(solution)/shard_map/ppermute | solution.py:22
  22.1 2.6 %collective-permute-start.12 = (bf16[48,1152]{1,0:T(8,128)(2,1)S(1)}, bf16[48,1152]{1,0:T(8,128)(2,1)S(1)}, u32[]{:S(2)}, u32[]{:S(2)}) collective-permute-start(bf16[48,1152]{1,0:T(8,128)(2,1)S(1)} %get-tuple-element.56), channel_id=1, source_target_pairs={{0,4},{1,5},{2,6},{3,7},{4,0},{5,1},{6,2},{7,3},{8,12},{9,13},{10,... | collective-permute-start | bytes 331784 | tf_op jit(solution)/shard_map/ppermute | solution.py:22
  24.7 1.3 collective-permute-start.13
  26.0 1.6 %collective-permute-start.14 = (bf16[48,1152]{1,0:T(8,128)(2,1)S(1)}, bf16[48,1152]{1,0:T(8,128)(2,1)S(1)}, u32[]{:S(2)}, u32[]{:S(2)}) collective-permute-start(bf16[48,1152]{1,0:T(8,128)(2,1)S(1)} %get-tuple-element.58), channel_id=1, source_target_pairs={{0,6},{1,7},{2,4},{3,5},{4,2},{5,3},{6,0},{7,1},{8,14},{9,15},{10,... | collective-permute-start | bytes 331784 | tf_op jit(solution)/shard_map/ppermute | solution.py:22
  27.9 8.8 %collective-permute-done.12.refs_8_.refs_0_ = bf16[48,1152]{1,0:T(8,128)(2,1)S(1)} collective-permute-done((bf16[48,1152]{1,0:T(8,128)(2,1)S(1)}, bf16[48,1152]{1,0:T(8,128)(2,1)S(1)}, u32[]{:S(2)}, u32[]{:S(2)}) %collective-permute-start.12) | collective-permute-done | bytes 110624 | tf_op jit(solution)/shard_map/ppermute | solution.py:22
  36.7 2.4 %collective-permute-done.13.refs_9_.refs_1_ = bf16[48,1152]{1,0:T(8,128)(2,1)S(1)} collective-permute-done((bf16[48,1152]{1,0:T(8,128)(2,1)S(1)}, bf16[48,1152]{1,0:T(8,128)(2,1)S(1)}, u32[]{:S(2)}, u32[]{:S(2)}) %collective-permute-start.13) | collective-permute-done | bytes 110624 | tf_op jit(solution)/shard_map/ppermute | solution.py:22
  39.1 0.5 adapter_rows.4.refs_4_
  39.6 0.6 collective-permute-start.20
  40.2 1.9 %collective-permute-done.14.refs_10_.refs_0_ = bf16[48,1152]{1,0:T(8,128)(2,1)S(1)} collective-permute-done((bf16[48,1152]{1,0:T(8,128)(2,1)S(1)}, bf16[48,1152]{1,0:T(8,128)(2,1)S(1)}, u32[]{:S(2)}, u32[]{:S(2)}) %collective-permute-start.14) | collective-permute-done | bytes 110624 | tf_op jit(solution)/shard_map/ppermute | solution.py:22
  42.1 2.5 %collective-permute-done.15.refs_11_.refs_1_ = bf16[48,1152]{1,0:T(8,128)(2,1)S(1)} collective-permute-done((bf16[48,1152]{1,0:T(8,128)(2,1)S(1)}, bf16[48,1152]{1,0:T(8,128)(2,1)S(1)}, u32[]{:S(2)}, u32[]{:S(2)}) %collective-permute-start.15) | collective-permute-done | bytes 110624 | tf_op jit(solution)/shard_map/ppermute | solution.py:22
  44.6 0.5 adapter_rows.5.refs_8_
  45.1 0.6 collective-permute-start.23
  45.7 0.5 collective-permute-start.18
  46.4 0.5 collective-permute-start.21
  46.9 4.3 %collective-permute-done.23.refs_10_ = bf16[96,1024]{1,0:T(8,128)(2,1)S(1)} collective-permute-done((bf16[96,1024]{1,0:T(8,128)(2,1)S(1)}, bf16[96,1024]{1,0:T(8,128)(2,1)S(1)}, u32[]{:S(2)}, u32[]{:S(2)}) %collective-permute-start.23) | collective-permute-done | bytes 196640 | tf_op jit(solution)/shard_map/ppermute | solution.py:22
  51.3 0.7 copy-done.1
  52.0 0.7 own_rows.1
  52.7 42.3 %expert_rows.1 = (bf16[2,192,1024]{2,1,0:T(8,128)(2,1)S(1)}, bf16[2,96,1024]{2,1,0:T(8,128)(2,1)S(1)}, bf16[2,96,1024]{2,1,0:T(8,128)(2,1)S(1)}, f32[2,192,1024]...) custom-call(s32[4]{0:T(128)S(1)} %iota_xor_fusion.offset_ref, ...), custom_call_target="tpu_custom_call" | custom-call | tf_op jit(solution)/shard_map/expert_rows/pallas_call | solution.py:177
  95.1 0.6 collective-permute-start.25
  96.1 2.0 %collective-permute-done.30.other_ref = bf16[2,96,1024]{2,1,0:T(8,128)(2,1)S(1)} collective-permute-done((bf16[2,96,1024]{2,1,0:T(8,128)(2,1)S(1)}, bf16[2,96,1024]{2,1,0:T(8,128)(2,1)S(1)}, u32[]{:S(2)}, u32[]{:S(2)}) %collective-permute-start.30) | collective-permute-done | bytes 393248 | tf_op jit(solution)/shard_map/ppermute | solution.py:22
  98.1 0.5 collective-permute-start.31
  98.7 1.6 %collective-permute-start.26 = (bf16[192,1024]{1,0:T(8,128)(2,1)S(1)}, bf16[192,1024]{1,0:T(8,128)(2,1)S(1)}, u32[]{:S(2)}, u32[]{:S(2)}) collective-permute-start(bf16[192,1024]{1,0:T(8,128)(2,1)S(1)} %fusion), channel_id=1, source_target_pairs={{0,16},{8,24},{16,0},{24,8},{1,17},{9,25},{17,1},{25,9},{2,18},{10... | collective-permute-start | bytes 1179656 | tf_op jit(solution)/shard_map/ppermute | solution.py:22
  100.4 0.5 collective-permute-start.35
  101.0 5.0 %collective-permute-done.31.refs_0_ = bf16[96,1024]{1,0:T(8,128)(2,1)S(1)} collective-permute-done((bf16[96,1024]{1,0:T(8,128)(2,1)S(1)}, bf16[96,1024]{1,0:T(8,128)(2,1)S(1)}, u32[]{:S(2)}, u32[]{:S(2)}) %collective-permute-start.31) | collective-permute-done | bytes 196640 | tf_op jit(solution)/shard_map/ppermute | solution.py:22
  106.0 3.8 %collective-permute-start.32 = (bf16[48,1024]{1,0:T(8,128)(2,1)S(1)}, bf16[48,1024]{1,0:T(8,128)(2,1)S(1)}, u32[]{:S(2)}, u32[]{:S(2)}) collective-permute-start(bf16[48,1024]{1,0:T(8,128)(2,1)S(1)} %get-tuple-element.71), channel_id=1, source_target_pairs={{0,4},{1,5},{2,6},{3,7},{4,0},{5,1},{6,2},{7,3},{8,12},{9,13},{10,... | collective-permute-start | bytes 294920 | tf_op jit(solution)/shard_map/ppermute | solution.py:22
  109.9 8.2 %collective-permute-done.35.refs_0_ = bf16[96,1024]{1,0:T(8,128)(2,1)S(1)} collective-permute-done((bf16[96,1024]{1,0:T(8,128)(2,1)S(1)}, bf16[96,1024]{1,0:T(8,128)(2,1)S(1)}, u32[]{:S(2)}, u32[]{:S(2)}) %collective-permute-start.35) | collective-permute-done | bytes 196640 | tf_op jit(solution)/shard_map/ppermute | solution.py:22
  118.8 3.5 %collective-permute-start.36 = (bf16[48,1024]{1,0:T(8,128)(2,1)S(1)}, bf16[48,1024]{1,0:T(8,128)(2,1)S(1)}, u32[]{:S(2)}, u32[]{:S(2)}) collective-permute-start(bf16[48,1024]{1,0:T(8,128)(2,1)S(1)} %get-tuple-element.75), channel_id=1, source_target_pairs={{0,6},{1,7},{2,4},{3,5},{4,2},{5,3},{6,0},{7,1},{8,14},{9,15},{10,... | collective-permute-start | bytes 294920 | tf_op jit(solution)/shard_map/ppermute | solution.py:22
  122.3 2.8 %collective-permute-start.37 = (bf16[48,1024]{1,0:T(8,128)(2,1)S(1)}, bf16[48,1024]{1,0:T(8,128)(2,1)S(1)}, u32[]{:S(2)}, u32[]{:S(2)}) collective-permute-start(bf16[48,1024]{1,0:T(8,128)(2,1)S(1)} %get-tuple-element.76), channel_id=1, source_target_pairs={{0,7},{1,6},{2,5},{3,4},{4,3},{5,2},{6,1},{7,0},{8,15},{9,14},{10,... | collective-permute-start | bytes 294920 | tf_op jit(solution)/shard_map/ppermute | solution.py:22
  125.1 1.5 %collective-permute-start.27 = (bf16[48,1024]{1,0:T(8,128)(2,1)S(1)}, bf16[48,1024]{1,0:T(8,128)(2,1)S(1)}, u32[]{:S(2)}, u32[]{:S(2)}) collective-permute-start(bf16[48,1024]{1,0:T(8,128)(2,1)S(1)} %get-tuple-element.66), channel_id=1, source_target_pairs={{0,1},{1,0},{2,3},{3,2},{4,5},{5,4},{6,7},{7,6},{8,9},{9,8},{10,11... | collective-permute-start | bytes 294920 | tf_op jit(solution)/shard_map/ppermute | solution.py:22
  126.6 1.8 %collective-permute-start.28 = (bf16[48,1024]{1,0:T(8,128)(2,1)S(1)}, bf16[48,1024]{1,0:T(8,128)(2,1)S(1)}, u32[]{:S(2)}, u32[]{:S(2)}) collective-permute-start(bf16[48,1024]{1,0:T(8,128)(2,1)S(1)} %get-tuple-element.67), channel_id=1, source_target_pairs={{0,2},{1,3},{2,0},{3,1},{4,6},{5,7},{6,4},{7,5},{8,10},{9,11},{10,... | collective-permute-start | bytes 294920 | tf_op jit(solution)/shard_map/ppermute | solution.py:22
  128.6 0.8 mix.1
  129.4 0.7 collective-permute-done.36.refs_6_
  130.1 2.2 %collective-permute-done.37.refs_7_ = bf16[48,1024]{1,0:T(8,128)(2,1)S(1)} collective-permute-done((bf16[48,1024]{1,0:T(8,128)(2,1)S(1)}, bf16[48,1024]{1,0:T(8,128)(2,1)S(1)}, u32[]{:S(2)}, u32[]{:S(2)}) %collective-permute-start.37) | collective-permute-done | bytes 98336 | tf_op jit(solution)/shard_map/ppermute | solution.py:22
  132.6 1.3 collective-permute-done.29.refs_3_
  133.9 1.2 finish.1
  (55 shorter events, 4.3 us)
Async XLA Ops:
  0.6 50.6 %copy-start = (bf16[4096,8]{0,1:T(8,128)(2,1)S(1)}, bf16[4096,8]{0,1:T(8,128)(2,1)}, u32[]{:S(2)}) copy-start(bf16[4096,8]{0,1:T(8,128)(2,1)} %param.16) | copy-start | bytes 196612
  4.2 3.5 %collective-permute-start.2 = (bf16[16,128]{1,0:T(8,128)(2,1)S(1)}, bf16[16,128]{1,0:T(8,128)(2,1)S(1)}, u32[]{:S(2)}, u32[]{:S(2)}) collective-permute-start(bf16[16,128]{1,0:T(8,128)(2,1)S(1)} %get-tuple-element.43.refs_0_), channel_id=1, source_target_pairs={{0,24},{8,16},{16,8},{24,0},{1,25},{9,17},{17,9},{25,1},{2,26},{10... | collective-permute-start | bytes 12296 | tf_op jit(solution)/shard_map/ppermute | solution.py:22
  5.1 3.6 %collective-permute-start.1 = (bf16[16,128]{1,0:T(8,128)(2,1)S(1)}, bf16[16,128]{1,0:T(8,128)(2,1)S(1)}, u32[]{:S(2)}, u32[]{:S(2)}) collective-permute-start(bf16[16,128]{1,0:T(8,128)(2,1)S(1)} %get-tuple-element.43.refs_0_), channel_id=1, source_target_pairs={{0,16},{8,24},{16,0},{24,8},{1,17},{9,25},{17,1},{25,9},{2,18},{10... | collective-permute-start | bytes 12296 | tf_op jit(solution)/shard_map/ppermute | solution.py:22
  5.8 3.0 %collective-permute-start = (bf16[16,128]{1,0:T(8,128)(2,1)S(1)}, bf16[16,128]{1,0:T(8,128)(2,1)S(1)}, u32[]{:S(2)}, u32[]{:S(2)}) collective-permute-start(bf16[16,128]{1,0:T(8,128)(2,1)S(1)} %get-tuple-element.43.refs_0_), channel_id=1, source_target_pairs={{0,8},{8,0},{16,24},{24,16},{1,9},{9,1},{17,25},{25,17},{2,10},{10... | collective-permute-start | bytes 12296 | tf_op jit(solution)/shard_map/ppermute | solution.py:22
  6.1 13.9 %collective-permute-start.3 = (bf16[128,1024]{1,0:T(8,128)(2,1)S(1)}, bf16[128,1024]{1,0:T(8,128)(2,1)S(1)}, u32[]{:S(2)}, u32[]{:S(2)}) collective-permute-start(bf16[128,1024]{1,0:T(8,128)(2,1)S(1)} %get-tuple-element.46), channel_id=1, source_target_pairs={{0,8},{8,0},{16,24},{24,16},{1,9},{9,1},{17,25},{25,17},{2,10},{10... | collective-permute-start | bytes 786440 | tf_op jit(solution)/shard_map/ppermute | solution.py:22
  6.3 13.7 %collective-permute-start.4 = (bf16[128,1024]{1,0:T(8,128)(2,1)S(1)}, bf16[128,1024]{1,0:T(8,128)(2,1)S(1)}, u32[]{:S(2)}, u32[]{:S(2)}) collective-permute-start(bf16[128,1024]{1,0:T(8,128)(2,1)S(1)} %get-tuple-element.47), channel_id=1, source_target_pairs={{0,16},{8,24},{16,0},{24,8},{1,17},{9,25},{17,1},{25,9},{2,18},{10... | collective-permute-start | bytes 786440 | tf_op jit(solution)/shard_map/ppermute | solution.py:22
  7.7 12.3 %collective-permute-start.5 = (bf16[128,1024]{1,0:T(8,128)(2,1)S(1)}, bf16[128,1024]{1,0:T(8,128)(2,1)S(1)}, u32[]{:S(2)}, u32[]{:S(2)}) collective-permute-start(bf16[128,1024]{1,0:T(8,128)(2,1)S(1)} %get-tuple-element.48), channel_id=1, source_target_pairs={{0,24},{8,16},{16,8},{24,0},{1,25},{9,17},{17,9},{25,1},{2,26},{10... | collective-permute-start | bytes 786440 | tf_op jit(solution)/shard_map/ppermute | solution.py:22
  9.2 5.2 %collective-permute-start.9 = (bf16[48,1152]{1,0:T(8,128)(2,1)S(1)}, bf16[48,1152]{1,0:T(8,128)(2,1)S(1)}, u32[]{:S(2)}, u32[]{:S(2)}) collective-permute-start(bf16[48,1152]{1,0:T(8,128)(2,1)S(1)} %get-tuple-element.53), channel_id=1, source_target_pairs={{0,1},{1,0},{2,3},{3,2},{4,5},{5,4},{6,7},{7,6},{8,9},{9,8},{10,11... | collective-permute-start | bytes 331784 | tf_op jit(solution)/shard_map/ppermute | solution.py:22
  11.4 4.8 %collective-permute-start.10 = (bf16[48,1152]{1,0:T(8,128)(2,1)S(1)}, bf16[48,1152]{1,0:T(8,128)(2,1)S(1)}, u32[]{:S(2)}, u32[]{:S(2)}) collective-permute-start(bf16[48,1152]{1,0:T(8,128)(2,1)S(1)} %get-tuple-element.54), channel_id=1, source_target_pairs={{0,2},{1,3},{2,0},{3,1},{4,6},{5,7},{6,4},{7,5},{8,10},{9,11},{10,... | collective-permute-start | bytes 331784 | tf_op jit(solution)/shard_map/ppermute | solution.py:22
  14.3 5.6 %collective-permute-start.11 = (bf16[48,1152]{1,0:T(8,128)(2,1)S(1)}, bf16[48,1152]{1,0:T(8,128)(2,1)S(1)}, u32[]{:S(2)}, u32[]{:S(2)}) collective-permute-start(bf16[48,1152]{1,0:T(8,128)(2,1)S(1)} %get-tuple-element.55), channel_id=1, source_target_pairs={{0,3},{1,2},{2,1},{3,0},{4,7},{5,6},{6,5},{7,4},{8,11},{9,10},{10,... | collective-permute-start | bytes 331784 | tf_op jit(solution)/shard_map/ppermute | solution.py:22
  20.7 25.0 %collective-permute-start.17 = (bf16[192,1024]{1,0:T(8,128)(2,1)S(1)}, bf16[192,1024]{1,0:T(8,128)(2,1)S(1)}, u32[]{:S(2)}, u32[]{:S(2)}) collective-permute-start(bf16[192,1024]{1,0:T(8,128)(2,1)S(1)} %adapter_rows.3.refs_0_), channel_id=1, source_target_pairs={{0,16},{8,24},{16,0},{24,8},{1,17},{9,25},{17,1},{25,9},{2,18},{10... | collective-permute-start | bytes 1179656 | tf_op jit(solution)/shard_map/ppermute | solution.py:22
  22.1 14.6 %collective-permute-start.12 = (bf16[48,1152]{1,0:T(8,128)(2,1)S(1)}, bf16[48,1152]{1,0:T(8,128)(2,1)S(1)}, u32[]{:S(2)}, u32[]{:S(2)}) collective-permute-start(bf16[48,1152]{1,0:T(8,128)(2,1)S(1)} %get-tuple-element.56), channel_id=1, source_target_pairs={{0,4},{1,5},{2,6},{3,7},{4,0},{5,1},{6,2},{7,3},{8,12},{9,13},{10,... | collective-permute-start | bytes 331784 | tf_op jit(solution)/shard_map/ppermute | solution.py:22
  24.7 14.4 %collective-permute-start.13 = (bf16[48,1152]{1,0:T(8,128)(2,1)S(1)}, bf16[48,1152]{1,0:T(8,128)(2,1)S(1)}, u32[]{:S(2)}, u32[]{:S(2)}) collective-permute-start(bf16[48,1152]{1,0:T(8,128)(2,1)S(1)} %get-tuple-element.57), channel_id=1, source_target_pairs={{0,5},{1,4},{2,7},{3,6},{4,1},{5,0},{6,3},{7,2},{8,13},{9,12},{10,... | collective-permute-start | bytes 331784 | tf_op jit(solution)/shard_map/ppermute | solution.py:22
  26.0 16.2 %collective-permute-start.14 = (bf16[48,1152]{1,0:T(8,128)(2,1)S(1)}, bf16[48,1152]{1,0:T(8,128)(2,1)S(1)}, u32[]{:S(2)}, u32[]{:S(2)}) collective-permute-start(bf16[48,1152]{1,0:T(8,128)(2,1)S(1)} %get-tuple-element.58), channel_id=1, source_target_pairs={{0,6},{1,7},{2,4},{3,5},{4,2},{5,3},{6,0},{7,1},{8,14},{9,15},{10,... | collective-permute-start | bytes 331784 | tf_op jit(solution)/shard_map/ppermute | solution.py:22
  27.5 17.1 %collective-permute-start.15 = (bf16[48,1152]{1,0:T(8,128)(2,1)S(1)}, bf16[48,1152]{1,0:T(8,128)(2,1)S(1)}, u32[]{:S(2)}, u32[]{:S(2)}) collective-permute-start(bf16[48,1152]{1,0:T(8,128)(2,1)S(1)} %get-tuple-element.59), channel_id=1, source_target_pairs={{0,7},{1,6},{2,5},{3,4},{4,3},{5,2},{6,1},{7,0},{8,15},{9,14},{10,... | collective-permute-start | bytes 331784 | tf_op jit(solution)/shard_map/ppermute | solution.py:22
  39.6 6.8 %collective-permute-start.20 = (bf16[96,1024]{1,0:T(8,128)(2,1)S(1)}, bf16[96,1024]{1,0:T(8,128)(2,1)S(1)}, u32[]{:S(2)}, u32[]{:S(2)}) collective-permute-start(bf16[96,1024]{1,0:T(8,128)(2,1)S(1)} %adapter_rows.4.refs_4_), channel_id=1, source_target_pairs={{0,16},{8,24},{16,0},{24,8},{1,17},{9,25},{17,1},{25,9},{2,18},{10... | collective-permute-start | bytes 589832 | tf_op jit(solution)/shard_map/ppermute | solution.py:22
  40.2 6.2 %collective-permute-start.19 = (bf16[96,1024]{1,0:T(8,128)(2,1)S(1)}, bf16[96,1024]{1,0:T(8,128)(2,1)S(1)}, u32[]{:S(2)}, u32[]{:S(2)}) collective-permute-start(bf16[96,1024]{1,0:T(8,128)(2,1)S(1)} %adapter_rows.4.refs_4_), channel_id=1, source_target_pairs={{0,8},{8,0},{16,24},{24,16},{1,9},{9,1},{17,25},{25,17},{2,10},{10... | collective-permute-start | bytes 589832 | tf_op jit(solution)/shard_map/ppermute | solution.py:22
  45.1 6.1 %collective-permute-start.23 = (bf16[96,1024]{1,0:T(8,128)(2,1)S(1)}, bf16[96,1024]{1,0:T(8,128)(2,1)S(1)}, u32[]{:S(2)}, u32[]{:S(2)}) collective-permute-start(bf16[96,1024]{1,0:T(8,128)(2,1)S(1)} %adapter_rows.5.refs_8_), channel_id=1, source_target_pairs={{0,16},{8,24},{16,0},{24,8},{1,17},{9,25},{17,1},{25,9},{2,18},{10... | collective-permute-start | bytes 589832 | tf_op jit(solution)/shard_map/ppermute | solution.py:22
  45.7 7.0 %collective-permute-start.16 = (bf16[192,1024]{1,0:T(8,128)(2,1)S(1)}, bf16[192,1024]{1,0:T(8,128)(2,1)S(1)}, u32[]{:S(2)}, u32[]{:S(2)}) collective-permute-start(bf16[192,1024]{1,0:T(8,128)(2,1)S(1)} %adapter_rows.3.refs_0_), channel_id=1, source_target_pairs={{0,8},{8,0},{16,24},{24,16},{1,9},{9,1},{17,25},{25,17},{2,10},{10... | collective-permute-start | bytes 1179656 | tf_op jit(solution)/shard_map/ppermute | solution.py:22
  45.7 7.0 %collective-permute-start.18 = (bf16[192,1024]{1,0:T(8,128)(2,1)S(1)}, bf16[192,1024]{1,0:T(8,128)(2,1)S(1)}, u32[]{:S(2)}, u32[]{:S(2)}) collective-permute-start(bf16[192,1024]{1,0:T(8,128)(2,1)S(1)} %collective-permute-done.17.refs_2_), channel_id=1, source_target_pairs={{0,8},{8,0},{16,24},{24,16},{1,9},{9,1},{17,25},{25,17},{2,10},{10... | collective-permute-start | bytes 1179656 | tf_op jit(solution)/shard_map/ppermute | solution.py:22
  46.4 6.3 %collective-permute-start.22 = (bf16[96,1024]{1,0:T(8,128)(2,1)S(1)}, bf16[96,1024]{1,0:T(8,128)(2,1)S(1)}, u32[]{:S(2)}, u32[]{:S(2)}) collective-permute-start(bf16[96,1024]{1,0:T(8,128)(2,1)S(1)} %adapter_rows.5.refs_8_), channel_id=1, source_target_pairs={{0,8},{8,0},{16,24},{24,16},{1,9},{9,1},{17,25},{25,17},{2,10},{10... | collective-permute-start | bytes 589832 | tf_op jit(solution)/shard_map/ppermute | solution.py:22
  46.4 6.3 %collective-permute-start.21 = (bf16[96,1024]{1,0:T(8,128)(2,1)S(1)}, bf16[96,1024]{1,0:T(8,128)(2,1)S(1)}, u32[]{:S(2)}, u32[]{:S(2)}) collective-permute-start(bf16[96,1024]{1,0:T(8,128)(2,1)S(1)} %collective-permute-done.20.refs_6_), channel_id=1, source_target_pairs={{0,8},{8,0},{16,24},{24,16},{1,9},{9,1},{17,25},{25,17},{2,10},{10... | collective-permute-start | bytes 589832 | tf_op jit(solution)/shard_map/ppermute | solution.py:22
  51.2 1.5 %collective-permute-start.24 = (bf16[96,1024]{1,0:T(8,128)(2,1)S(1)}, bf16[96,1024]{1,0:T(8,128)(2,1)S(1)}, u32[]{:S(2)}, u32[]{:S(2)}) collective-permute-start(bf16[96,1024]{1,0:T(8,128)(2,1)S(1)} %collective-permute-done.23.refs_10_), channel_id=1, source_target_pairs={{0,8},{8,0},{16,24},{24,16},{1,9},{9,1},{17,25},{25,17},{2,10},{10... | collective-permute-start | bytes 589832 | tf_op jit(solution)/shard_map/ppermute | solution.py:22
  51.3 0.7 copy-start.1
  95.1 3.6 %collective-permute-start.25 = (bf16[2,192,1024]{2,1,0:T(8,128)(2,1)S(1)}, bf16[2,192,1024]{2,1,0:T(8,128)(2,1)S(1)}, u32[]{:S(2)}, u32[]{:S(2)}) collective-permute-start(bf16[2,192,1024]{2,1,0:T(8,128)(2,1)S(1)} %get-tuple-element.64), channel_id=1, source_target_pairs={{0,8},{8,0},{16,24},{24,16},{1,9},{9,1},{17,25},{25,17},{2,10},{10... | collective-permute-start | bytes 2359304 | tf_op jit(solution)/shard_map/ppermute | solution.py:22
  95.6 2.5 %collective-permute-start.30 = (bf16[2,96,1024]{2,1,0:T(8,128)(2,1)S(1)}, bf16[2,96,1024]{2,1,0:T(8,128)(2,1)S(1)}, u32[]{:S(2)}, u32[]{:S(2)}) collective-permute-start(bf16[2,96,1024]{2,1,0:T(8,128)(2,1)S(1)} %get-tuple-element.70), channel_id=1, source_target_pairs={{0,8},{8,0},{16,24},{24,16},{1,9},{9,1},{17,25},{25,17},{2,10},{10... | collective-permute-start | bytes 1179656 | tf_op jit(solution)/shard_map/ppermute | solution.py:22
  95.7 4.7 %collective-permute-start.34 = (bf16[2,96,1024]{2,1,0:T(8,128)(2,1)S(1)}, bf16[2,96,1024]{2,1,0:T(8,128)(2,1)S(1)}, u32[]{:S(2)}, u32[]{:S(2)}) collective-permute-start(bf16[2,96,1024]{2,1,0:T(8,128)(2,1)S(1)} %get-tuple-element.74), channel_id=1, source_target_pairs={{0,8},{8,0},{16,24},{24,16},{1,9},{9,1},{17,25},{25,17},{2,10},{10... | collective-permute-start | bytes 1179656 | tf_op jit(solution)/shard_map/ppermute | solution.py:22
  98.1 7.8 %collective-permute-start.31 = (bf16[96,1024]{1,0:T(8,128)(2,1)S(1)}, bf16[96,1024]{1,0:T(8,128)(2,1)S(1)}, u32[]{:S(2)}, u32[]{:S(2)}) collective-permute-start(bf16[96,1024]{1,0:T(8,128)(2,1)S(1)} %fusion.1), channel_id=1, source_target_pairs={{0,16},{8,24},{16,0},{24,8},{1,17},{9,25},{17,1},{25,9},{2,18},{10... | collective-permute-start | bytes 589832 | tf_op jit(solution)/shard_map/ppermute | solution.py:22
  98.7 19.8 %collective-permute-start.26 = (bf16[192,1024]{1,0:T(8,128)(2,1)S(1)}, bf16[192,1024]{1,0:T(8,128)(2,1)S(1)}, u32[]{:S(2)}, u32[]{:S(2)}) collective-permute-start(bf16[192,1024]{1,0:T(8,128)(2,1)S(1)} %fusion), channel_id=1, source_target_pairs={{0,16},{8,24},{16,0},{24,8},{1,17},{9,25},{17,1},{25,9},{2,18},{10... | collective-permute-start | bytes 1179656 | tf_op jit(solution)/shard_map/ppermute | solution.py:22
  100.4 17.7 %collective-permute-start.35 = (bf16[96,1024]{1,0:T(8,128)(2,1)S(1)}, bf16[96,1024]{1,0:T(8,128)(2,1)S(1)}, u32[]{:S(2)}, u32[]{:S(2)}) collective-permute-start(bf16[96,1024]{1,0:T(8,128)(2,1)S(1)} %fusion.2), channel_id=1, source_target_pairs={{0,16},{8,24},{16,0},{24,8},{1,17},{9,25},{17,1},{25,9},{2,18},{10... | collective-permute-start | bytes 589832 | tf_op jit(solution)/shard_map/ppermute | solution.py:22
  106.0 20.5 %collective-permute-start.32 = (bf16[48,1024]{1,0:T(8,128)(2,1)S(1)}, bf16[48,1024]{1,0:T(8,128)(2,1)S(1)}, u32[]{:S(2)}, u32[]{:S(2)}) collective-permute-start(bf16[48,1024]{1,0:T(8,128)(2,1)S(1)} %get-tuple-element.71), channel_id=1, source_target_pairs={{0,4},{1,5},{2,6},{3,7},{4,0},{5,1},{6,2},{7,3},{8,12},{9,13},{10,... | collective-permute-start | bytes 294920 | tf_op jit(solution)/shard_map/ppermute | solution.py:22
  109.8 18.6 %collective-permute-start.33 = (bf16[48,1024]{1,0:T(8,128)(2,1)S(1)}, bf16[48,1024]{1,0:T(8,128)(2,1)S(1)}, u32[]{:S(2)}, u32[]{:S(2)}) collective-permute-start(bf16[48,1024]{1,0:T(8,128)(2,1)S(1)} %get-tuple-element.72), channel_id=1, source_target_pairs={{0,5},{1,4},{2,7},{3,6},{4,1},{5,0},{6,3},{7,2},{8,13},{9,12},{10,... | collective-permute-start | bytes 294920 | tf_op jit(solution)/shard_map/ppermute | solution.py:22
  109.9 8.9 %collective-permute-start.8 = (f32[16,128]{1,0:T(8,128)S(1)}, f32[16,128]{1,0:T(8,128)S(1)}, u32[]{:S(2)}, u32[]{:S(2)}) collective-permute-start(f32[16,128]{1,0:T(8,128)S(1)} %get-tuple-element.51.refs_0_), channel_id=1, source_target_pairs={{0,24},{8,16},{16,8},{24,0},{1,25},{9,17},{17,9},{25,1},{2,26},{10... | collective-permute-start | bytes 24584 | tf_op jit(solution)/shard_map/ppermute | solution.py:22
  118.1 4.2 %collective-permute-start.7 = (f32[16,128]{1,0:T(8,128)S(1)}, f32[16,128]{1,0:T(8,128)S(1)}, u32[]{:S(2)}, u32[]{:S(2)}) collective-permute-start(f32[16,128]{1,0:T(8,128)S(1)} %get-tuple-element.51.refs_0_), channel_id=1, source_target_pairs={{0,16},{8,24},{16,0},{24,8},{1,17},{9,25},{17,1},{25,9},{2,18},{10... | collective-permute-start | bytes 24584 | tf_op jit(solution)/shard_map/ppermute | solution.py:22
  118.6 6.5 %collective-permute-start.6 = (f32[16,128]{1,0:T(8,128)S(1)}, f32[16,128]{1,0:T(8,128)S(1)}, u32[]{:S(2)}, u32[]{:S(2)}) collective-permute-start(f32[16,128]{1,0:T(8,128)S(1)} %get-tuple-element.51.refs_0_), channel_id=1, source_target_pairs={{0,8},{8,0},{16,24},{24,16},{1,9},{9,1},{17,25},{25,17},{2,10},{10... | collective-permute-start | bytes 24584 | tf_op jit(solution)/shard_map/ppermute | solution.py:22
  118.8 11.4 %collective-permute-start.36 = (bf16[48,1024]{1,0:T(8,128)(2,1)S(1)}, bf16[48,1024]{1,0:T(8,128)(2,1)S(1)}, u32[]{:S(2)}, u32[]{:S(2)}) collective-permute-start(bf16[48,1024]{1,0:T(8,128)(2,1)S(1)} %get-tuple-element.75), channel_id=1, source_target_pairs={{0,6},{1,7},{2,4},{3,5},{4,2},{5,3},{6,0},{7,1},{8,14},{9,15},{10,... | collective-permute-start | bytes 294920 | tf_op jit(solution)/shard_map/ppermute | solution.py:22
  122.3 10.1 %collective-permute-start.37 = (bf16[48,1024]{1,0:T(8,128)(2,1)S(1)}, bf16[48,1024]{1,0:T(8,128)(2,1)S(1)}, u32[]{:S(2)}, u32[]{:S(2)}) collective-permute-start(bf16[48,1024]{1,0:T(8,128)(2,1)S(1)} %get-tuple-element.76), channel_id=1, source_target_pairs={{0,7},{1,6},{2,5},{3,4},{4,3},{5,2},{6,1},{7,0},{8,15},{9,14},{10,... | collective-permute-start | bytes 294920 | tf_op jit(solution)/shard_map/ppermute | solution.py:22
  125.1 7.3 %collective-permute-start.27 = (bf16[48,1024]{1,0:T(8,128)(2,1)S(1)}, bf16[48,1024]{1,0:T(8,128)(2,1)S(1)}, u32[]{:S(2)}, u32[]{:S(2)}) collective-permute-start(bf16[48,1024]{1,0:T(8,128)(2,1)S(1)} %get-tuple-element.66), channel_id=1, source_target_pairs={{0,1},{1,0},{2,3},{3,2},{4,5},{5,4},{6,7},{7,6},{8,9},{9,8},{10,11... | collective-permute-start | bytes 294920 | tf_op jit(solution)/shard_map/ppermute | solution.py:22
  126.6 6.0 %collective-permute-start.28 = (bf16[48,1024]{1,0:T(8,128)(2,1)S(1)}, bf16[48,1024]{1,0:T(8,128)(2,1)S(1)}, u32[]{:S(2)}, u32[]{:S(2)}) collective-permute-start(bf16[48,1024]{1,0:T(8,128)(2,1)S(1)} %get-tuple-element.67), channel_id=1, source_target_pairs={{0,2},{1,3},{2,0},{3,1},{4,6},{5,7},{6,4},{7,5},{8,10},{9,11},{10,... | collective-permute-start | bytes 294920 | tf_op jit(solution)/shard_map/ppermute | solution.py:22
  128.4 5.5 %collective-permute-start.29 = (bf16[48,1024]{1,0:T(8,128)(2,1)S(1)}, bf16[48,1024]{1,0:T(8,128)(2,1)S(1)}, u32[]{:S(2)}, u32[]{:S(2)}) collective-permute-start(bf16[48,1024]{1,0:T(8,128)(2,1)S(1)} %get-tuple-element.68), channel_id=1, source_target_pairs={{0,3},{1,2},{2,1},{3,0},{4,7},{5,6},{6,5},{7,4},{8,11},{9,10},{10,... | collective-permute-start | bytes 294920 | tf_op jit(solution)/shard_map/ppermute | solution.py:22
